TPU v7x, 32 devices: a whole 2x2x4 slice. The times are simulated.
32 devices in a mesh: sub: 2 (over y), blk: 16 (over z, x, core).
Axes of the slice: x: 2, y: 2, z: 4, core: 2. Of those that a mesh axis runs over, the one named last changes fastest.
Arguments:
- queries: float32 [256, 1024], P('blk', 'sub'), may hold values from -0.2 to 0.2
- centroids: float32 [64, 16, 256], P('sub'), may hold values from -0.2 to 0.2
- code_ids: int32 [64, 8192], P('sub', 'blk'), may hold values from 0 to 255
- query_order: int32 [256], replicated, may hold values from 0 to 255, each once
Outputs:
- distances: float32 [256, 8192], P('sub', 'blk')
Inputs may be any that keep to these rules, and one draw needn't show every extreme that they name: query_order is a permutation of the query numbers.
All inputs are finite; a program needn't handle non-finite values.
Results may differ from a plain program's by a relative error of at most 0.00039.
Values may be sent and summed in bfloat16 or wider, within the bound.
No kernel may reach another device: no remote copies, remote signals or barrier semaphores. Data moves between devices by JAX's collectives and lax.ppermute only.
A program may use at most 128 MiB of HBM per device.

v0:
```python
import jax
import jax.numpy as jnp
from jax import lax
from jax.sharding import PartitionSpec as P


def build_tables(query_rows, centroids):
    local_spaces, sub_width, centers = centroids.shape
    count = query_rows.shape[0]
    split_rows = query_rows.reshape(count, local_spaces, sub_width)
    total = jnp.zeros((count, local_spaces, centers), jnp.float32)
    for column in range(sub_width):
        offset = split_rows[:, :, column, None] - centroids[None, :, column, :]
        total = total + offset * offset
    return total.astype(jnp.bfloat16).reshape(count, local_spaces * centers)


def make_onehot(code_ids, centers):
    labels = jnp.arange(centers, dtype=jnp.int32)
    onehot_codes = (code_ids[:, None, :] == labels[None, :, None]).astype(jnp.bfloat16)
    return onehot_codes.reshape(code_ids.shape[0] * centers, code_ids.shape[1])


def local(queries, centroids, code_ids, query_order):
    local_spaces, sub_width, centers = centroids.shape
    onehot_codes = make_onehot(code_ids, centers)
    partial_value = jnp.dot(
        build_tables(lax.all_gather(queries, "blk", axis=0, tiled=True), centroids),
        onehot_codes,
        preferred_element_type=jnp.float32,
    )
    ordered = jnp.take(partial_value, query_order, axis=0)
    return lax.psum_scatter(ordered, "sub", scatter_dimension=0, tiled=True)


def solution(mesh):
    in_specs = (P("blk", "sub"), P("sub", None, None), P("sub", "blk"), P())
    out_specs = P("sub", "blk")
    return jax.shard_map(local, mesh=mesh, in_specs=in_specs, out_specs=out_specs, check_vma=False)
```

profile of v0, /device:TPU:0, one launch (start us, length us, event | category | flops | bytes accessed | tf_op | source)
XLA Modules:
  0.0 82.1 jit_solution(4421742045267421387)
XLA Ops:
  6.5 0.0 reduce-scatter.2.cloned.1.call-start
  6.5 0.7 compare_select_fusion
  7.2 0.7 compare_and_fusion
  7.9 24.8 %all_gather.3 = f32[256,512]{1,0:T(8,128)S(1)} all-gather(f32[16,512]{1,0:T(8,128)} %param.4), channel_id=1, replica_groups=mesh['sub'=2,'blk'=16] {'blk'}, dimensions={0}, use_global_device_ids=true | all-gather | bytes 557056 | tf_op jit(solution)/shard_map/all_gather | solution.py:28
  32.7 0.2 copy.38
  32.9 0.5 fusion.35
  33.4 0.0 copy-start
  33.4 3.2 %fusion.36 = (f32[32,1,256]{2,1,0:T(1,128)S(1)}, f32[32,1,256]{2,1,0:T(1,128)S(1)}, f32[32,1,256]{2,1,0:T(1,128)S(1)}, f32[32,1,256]{2,1,0:T(1,128)S(1)}, f32[32...) fusion(f32[32,16,256]{2,1,0:T(8,128)} %param.5), kind=kLoop, calls=%fused_computation.75 | loop fusion | bytes 1048576 | tf_op jit(solution)/shard_map/slice | solution.py:13
  36.9 21.7 %add_convert_fusion.7 = bf16[256,32,256]{2,0,1:T(8,128)(2,1)S(1)} fusion(f32[32,256]{1,0:T(8,128)S(1)} %get-tuple-element.37, f32[256,32]{0,1:T(8,128)S(1)} %get-tuple-element.53, f32[32,256]{1,0:T(8,128)S(1)} %get-tuple-element.38, f32[256,32]{0,1:T(8,128)S(1)} %get-tuple-element.54, f32[32,256]{1,0:T(8,128)S(1)} %get-tuple-element.39, ...), kind=kLoop, calls=%fused_computation.4.clone.clone.clone.clone.2 | loop fusion | flops 100663296 | bytes 5242880 | tf_op jit(solution)/shard_map/dot_general | solution.py:27
  58.6 0.0 copy-done
  58.6 2.6 %fusion.34 = f32[256,512]{1,0:T(8,128)S(1)} fusion(s32[32,512]{1,0:T(8,128)S(1)} %copy-done, bf16[256,32,256]{2,0,1:T(8,128)(2,1)S(1)} %add_convert_fusion.7), kind=kOutput, calls=%fused_computation.37 | convolution fusion | flops 2151677952 | bytes 4784128 | tf_op jit(solution)/shard_map/dot_general | solution.py:27
  61.3 1.0 %gather_fusion = f32[256,512]{1,0:T(8,128)S(1)} fusion(f32[256,512]{1,0:T(8,128)S(1)} %fusion.34, s32[1024]{0:T(1024)S(1)} %pad_clamp_fusion), kind=kCustom, calls=%fused_computation | custom fusion | bytes 1049600 | tf_op jit(solution)/shard_map/jit(_take)/gather | solution.py:32
  62.2 0.9 %broadcast_select_fusion = f32[256,512]{1,0:T(8,128)} fusion(f32[256,512]{1,0:T(8,128)S(1)} %gather_fusion, pred[256]{0:T(512)(128)(4,1)S(1)} %compare_and_fusion), kind=kLoop, calls=%fused_computation.38 | loop fusion | flops 131072 | bytes 1048832 | tf_op jit(solution)/shard_map/jit(_take)/select_n | solution.py:32
  63.2 0.0 reduce-scatter.2.cloned.1.call-update
  63.2 12.1 %reduce-scatter.2.cloned.1.call-done = f32[128,512]{1,0:T(8,128)} async-done(((f32[256,512]{1,0:T(8,128)}), f32[128,512]{1,0:T(8,128)}) %reduce-scatter.2.cloned.1.call-update) | async-done | bytes 262160 | tf_op jit(solution)/shard_map/reduce_scatter | solution.py:33
  (17 shorter events, 0.1 us)
Async XLA Ops:
  6.5 68.7 %reduce-scatter.2.cloned.1.call-start = ((), (), s32[]{:S(2)}) async-start(), calls=%async_computation.1 | async-start | bytes 786432 | tf_op jit(solution)/shard_map/reduce_scatter | solution.py:33
  33.4 25.2 %copy-start = (s32[32,512]{1,0:T(8,128)S(1)}, s32[32,512]{1,0:T(8,128)}, u32[]{:S(2)}) copy-start(s32[32,512]{1,0:T(8,128)} %param.6) | copy-start | bytes 196612
Sparse Core Ops, SparseCore 0:
  63.3 11.9 reduce-scatter.1
where the time goes:
time: 82.3 us; the launch traced here: 82.1 us
  blocking collectives  24.8 us (30%)
  other arithmetic  24 us (29%)
  between operations  13.6 us (17%)
  waiting for transfers between devices  12.1 us (15%)
  local copies, waits for them, and re-layouts  4.99 us (6%)
  matrix products  2.64 us (3%)
    all_gather x1, blocking collectives, local(): lax.all_gather(queries, 'blk', axis=0, tiled=True)  24.8 us
    dot_general x1, other arithmetic, local(): jnp.dot(build_tables(lax.all_gather(queries, 'blk', axis=0, tiled=True),...  21.7 us
    reduce_scatter x1, waiting for transfers between devices, local(): return lax.psum_scatter(ordered, 'sub', scatter_dimension=0, tiled=True)  12.1 us
    slice x2, local copies, waits for them, and re-layouts, build_tables(): offset = split_rows[:, :, column, None] - centroids[None, :, column, :]  3.7 us
    dot_general x1, matrix products, local(): jnp.dot(build_tables(lax.all_gather(queries, 'blk', axis=0, tiled=True),...  2.64 us
  transfers between devices with their start and end apart: 1, of which 1 were waited for; matrix products, arithmetic and copies ran while one was open for 0% of the time, Pallas kernels for 0%

commit v1 on v0

v1 whole, which is shorter than its diff:
```python
import jax
import jax.numpy as jnp
from jax import lax
from jax.experimental import pallas as pl
from jax.experimental.pallas import tpu as pltpu
from jax.sharding import PartitionSpec as P

LANES = 128


def decode_kernel(codes_ref, centroids_ref, high_ref, low_ref, norm_ref):
    spaces, width, centers = centroids_ref.shape
    count = codes_ref.shape[1]
    norm_ref[...] = jnp.zeros(norm_ref.shape, jnp.float32)

    def some_spaces(group, carry):
        for tile in range(count // LANES):
            lanes = pl.ds(tile * LANES, LANES)
            code_rows = codes_ref[pl.ds(pl.multiple_of(group * 8, 8), 8), lanes]
            squares = jnp.zeros((8, LANES), jnp.float32)
            for member in range(8):
                space = group * 8 + member
                codes = jnp.broadcast_to(code_rows[member : member + 1], (8, LANES))
                within = codes & (LANES - 1)
                part = codes >> (LANES.bit_length() - 1)
                pieces = []
                for row in range(0, width, 8):
                    value = None
                    for piece in range(centers // LANES):
                        table = centroids_ref[space, pl.ds(row, 8), pl.ds(piece * LANES, LANES)]
                        found = jnp.take_along_axis(table, within, axis=1)
                        value = found if piece == 0 else jnp.where(part == piece, found, value)
                    squares = squares + value * value
                    pieces.append(value)
                values = jnp.concatenate(pieces, axis=0)
                high = values.astype(jnp.bfloat16)
                rows = pl.ds(pl.multiple_of(space * width, width), width)
                high_ref[rows, lanes] = high
                low_ref[rows, lanes] = (values - high.astype(jnp.float32)).astype(jnp.bfloat16)
            norm_ref[:, lanes] += squares
        return carry

    lax.fori_loop(0, spaces // 8, some_spaces, 0)


def decode(code_ids, centroids):
    spaces, width, centers = centroids.shape
    count = code_ids.shape[1]
    return pl.pallas_call(
        decode_kernel,
        out_shape=(
            jax.ShapeDtypeStruct((spaces * width, count), jnp.bfloat16),
            jax.ShapeDtypeStruct((spaces * width, count), jnp.bfloat16),
            jax.ShapeDtypeStruct((8, count), jnp.float32),
        ),
        name="decode",
    )(code_ids, centroids)


def distance_kernel(own_rows, masks, other, order_ref, queries_ref, high_ref, low_ref, norm_ref, out_ref):
    half = lax.axis_index("sub")
    if other:
        half = 1 - half
    own = lax.axis_index("blk")
    rows = out_ref.shape[0]
    total = queries_ref.shape[0]
    order = order_ref[pl.ds(half, 1), :]
    place = lax.broadcasted_iota(jnp.int32, (total, rows), 0)
    slot = place // own_rows
    holder = jnp.full(place.shape, own, jnp.int32)
    for bit, mask in enumerate(masks):
        holder = holder ^ (((slot >> bit) & 1) * mask)
    name = holder * own_rows + place % own_rows
    pick = jnp.where(name == order, 1.0, 0.0).astype(jnp.bfloat16)
    picked = lax.dot_general(pick, queries_ref[...], (((0,), (0,)), ((), ())), preferred_element_type=jnp.float32)
    query_norm = jnp.sum(picked * picked, axis=1, keepdims=True)
    left = (picked * -2.0).astype(jnp.bfloat16)
    cross = jnp.dot(left, high_ref[...], preferred_element_type=jnp.float32)
    cross = cross + jnp.dot(left, low_ref[...], preferred_element_type=jnp.float32)
    code_norm = jnp.sum(norm_ref[...], axis=0, keepdims=True)
    out_ref[...] = cross + (query_norm + code_norm)


def distances_of(other, own_rows, masks, order, queries, high, low, norm):
    rows = order.shape[1]
    return pl.pallas_call(
        lambda *refs: distance_kernel(own_rows, masks, other, *refs),
        out_shape=jax.ShapeDtypeStruct((rows, high.shape[1]), jnp.float32),
        name="theirs" if other else "mine",
    )(order, queries, high, low, norm)


def solution(mesh):
    blocks = mesh.shape["blk"]
    halves = mesh.shape["sub"]
    masks = []
    while (1 << len(masks)) < blocks:
        masks.append(blocks >> (len(masks) + 1))

    def local(queries, centroids, code_ids, query_order):
        own_rows = queries.shape[0]
        order = query_order.reshape(halves, -1)
        rows = queries.astype(jnp.bfloat16)
        for mask in masks:
            rows = jnp.concatenate([rows, lax.ppermute(rows, "blk", [(i, i ^ mask) for i in range(blocks)])], axis=0)
        high, low, norm = decode(code_ids, centroids)
        theirs = distances_of(True, own_rows, masks, order, rows, high, low, norm)
        arrived = lax.ppermute(theirs, "sub", [(i, i ^ 1) for i in range(halves)])
        mine = distances_of(False, own_rows, masks, order, rows, high, low, norm)
        return mine + arrived

    in_specs = (P("blk", "sub"), P("sub", None, None), P("sub", "blk"), P())
    return jax.shard_map(local, mesh=mesh, in_specs=in_specs, out_specs=P("sub", "blk"), check_vma=False)
```

time: 82.3 us -> 31.3 us (0.38)
  blocking collectives: 24.8 us -> 0 us
  other arithmetic: 24 us -> 2.47 us
  between operations: 13.6 us -> 0.05 us
  starting transfers between devices: 0.01 us -> 9.12 us
  Pallas kernels: 0 us -> 8.38 us
  local copies, waits for them, and re-layouts: 4.99 us -> 0.72 us
  matrix products: 2.64 us -> 0 us
  waiting for transfers between devices: 12.1 us -> 10.3 us
    all_gather x1 -> x0, blocking collectives: 24.8 us -> none  [local(): lax.all_gather(queries, 'blk', axis=0, tiled=True)]
    dot_general x1 -> x0, other arithmetic: 21.7 us -> none  [local(): jnp.dot(build_tables(lax.all_gather(queries, 'blk', axis=0, tiled=True),...]
    reduce_scatter x1 -> x0, waiting for transfers between devices: 12.1 us -> none  [local(): return lax.psum_scatter(ordered, 'sub', scatter_dimension=0, tiled=True)]
    ppermute x0 -> x5, waiting for transfers between devices: none -> 10.3 us  [the longest x4 5.8 us: local(): lax.ppermute(rows, 'blk', [(i, i ^ mask) for i in range(blocks)])]
    ppermute x0 -> x5, starting transfers between devices: none -> 9.12 us  [the longest x4 7.6 us: local(): lax.ppermute(rows, 'blk', [(i, i ^ mask) for i in range(blocks)])]
    pallas_call x0 -> x3, Pallas kernels: none -> 8.38 us  [the longest x2 5.09 us: distances_of(): pl.pallas_call(lambda *refs: distance_kernel(own_rows, masks, other, *ref...]
    slice x2 -> x0, local copies, waits for them, and re-layouts: 3.7 us -> none  [build_tables(): offset = split_rows[:, :, column, None] - centroids[None, :, column, :]]
    dot_general x1 -> x0, matrix products: 2.64 us -> none  [local(): jnp.dot(build_tables(lax.all_gather(queries, 'blk', axis=0, tiled=True),...]
  transfers between devices with their start and end apart: 1 -> 5, of which waited for: 1 -> 4; matrix products, arithmetic and copies ran while one was open for 0% -> 0% of each run, Pallas kernels for 0% -> 19%
where the time goes in v1:
time: 31.3 us; the launch traced here: 31 us
  waiting for transfers between devices  10.3 us (33%)
  starting transfers between devices  9.12 us (29%)
  Pallas kernels  8.38 us (27%)
  other arithmetic  2.47 us (8%)
  local copies, waits for them, and re-layouts  0.72 us (2%)
    ppermute x4, starting transfers between devices, local(): lax.ppermute(rows, 'blk', [(i, i ^ mask) for i in range(blocks)])  7.6 us
    ppermute x4, waiting for transfers between devices, local(): lax.ppermute(rows, 'blk', [(i, i ^ mask) for i in range(blocks)])  5.8 us
    pallas_call x2, Pallas kernels, distances_of(): pl.pallas_call(lambda *refs: distance_kernel(own_rows, masks, other, *ref...  5.09 us
    ppermute x1, waiting for transfers between devices, local(): arrived = lax.ppermute(theirs, 'sub', [(i, i ^ 1) for i in range(halves)])  4.5 us
    pallas_call x1, Pallas kernels, decode(): pl.pallas_call(decode_kernel, out_shape=(jax.ShapeDtypeStruct((spaces * w...  3.28 us
    add x1, other arithmetic, local(): return mine + arrived  1.69 us
    ppermute x1, starting transfers between devices, local(): arrived = lax.ppermute(theirs, 'sub', [(i, i ^ 1) for i in range(halves)])  1.52 us
    unnamed x1, other arithmetic  0.76 us
  transfers between devices with their start and end apart: 5, of which 4 were waited for; matrix products, arithmetic and copies ran while one was open for 0% of the time, Pallas kernels for 19%

profile of v1, /device:TPU:0, one launch (start us, length us, event | category | flops | bytes accessed | tf_op | source)
XLA Modules:
  0.0 31.0 jit_solution(1977497925918507293)
XLA Ops:
  0.0 0.8 %constant_dynamic-update-slice_fusion.4 = (bf16[256,512]{1,0:T(8,128)(2,1)S(1)}, bf16[16,512]{1,0:T(8,128)(2,1)S(1)}) fusion(f32[16,512]{1,0:T(8,128)} %param.4), kind=kLoop, calls=%fused_computation.7 | loop fusion | flops 8191 | bytes 65536
  0.8 4.1 %collective-permute-start = (bf16[16,512]{1,0:T(8,128)(2,1)S(1)}, bf16[16,512]{1,0:T(8,128)(2,1)S(1)}, u32[]{:S(2)}, u32[]{:S(2)}) collective-permute-start(bf16[16,512]{1,0:T(8,128)(2,1)S(1)} %get-tuple-element.12), channel_id=1, source_target_pairs={{0,8},{1,9},{2,10},{3,11},{4,12},{5,13},{6,14},{7,15},{8,0},{9,1},... | collective-permute-start | bytes 49160 | tf_op jit(solution)/shard_map/ppermute | solution.py:105
  4.8 1.7 %collective-permute-done = bf16[16,512]{1,0:T(8,128)(2,1)S(1)} collective-permute-done((bf16[16,512]{1,0:T(8,128)(2,1)S(1)}, bf16[16,512]{1,0:T(8,128)(2,1)S(1)}, u32[]{:S(2)}, u32[]{:S(2)}) %collective-permute-start) | collective-permute-done | bytes 16416 | tf_op jit(solution)/shard_map/ppermute | solution.py:105
  6.5 1.9 %collective-permute-start.1 = (bf16[32,512]{1,0:T(8,128)(2,1)S(1)}, bf16[32,512]{1,0:T(8,128)(2,1)S(1)}, u32[]{:S(2)}, u32[]{:S(2)}) collective-permute-start(bf16[32,512]{1,0:T(8,128)(2,1)S(1)} %pad_maximum_fusion.2), channel_id=1, source_target_pairs={{0,4},{1,5},{2,6},{3,7},{4,0},{5,1},{6,2},{7,3},{8,12},{9,13},{10,... | collective-permute-start | bytes 98312 | tf_op jit(solution)/shard_map/ppermute | solution.py:105
  8.5 3.3 %decode.1 = (bf16[512,512]{1,0:T(8,128)(2,1)}, bf16[512,512]{1,0:T(8,128)(2,1)}, f32[8,512]{1,0:T(8,128)}) custom-call(s32[32,512]{1,0:T(8,128)} %codes_ref.1, f32[32,16,256]{2,1,0:T(8,128)} %centroids_ref.1), custom_call_target="tpu_custom_call" | custom-call | tf_op jit(solution)/shard_map/decode/pallas_call | solution.py:49
  11.7 0.0 collective-permute-done.1
  11.8 1.6 %collective-permute-start.2 = (bf16[64,512]{1,0:T(8,128)(2,1)S(1)}, bf16[64,512]{1,0:T(8,128)(2,1)S(1)}, u32[]{:S(2)}, u32[]{:S(2)}) collective-permute-start(bf16[64,512]{1,0:T(8,128)(2,1)S(1)} %pad_maximum_fusion.1), channel_id=1, source_target_pairs={{0,2},{1,3},{2,0},{3,1},{4,6},{5,7},{6,4},{7,5},{8,10},{9,11},{10,... | collective-permute-start | bytes 196616 | tf_op jit(solution)/shard_map/ppermute | solution.py:105
  13.3 2.8 %collective-permute-done.2 = bf16[64,512]{1,0:T(8,128)(2,1)S(1)} collective-permute-done((bf16[64,512]{1,0:T(8,128)(2,1)S(1)}, bf16[64,512]{1,0:T(8,128)(2,1)S(1)}, u32[]{:S(2)}, u32[]{:S(2)}) %collective-permute-start.2) | collective-permute-done | bytes 65568 | tf_op jit(solution)/shard_map/ppermute | solution.py:105
  16.1 0.1 collective-permute-start.3
  16.2 1.3 %collective-permute-done.3 = bf16[128,512]{1,0:T(8,128)(2,1)S(1)} collective-permute-done((bf16[128,512]{1,0:T(8,128)(2,1)S(1)}, bf16[128,512]{1,0:T(8,128)(2,1)S(1)}, u32[]{:S(2)}, u32[]{:S(2)}) %collective-permute-start.3) | collective-permute-done | bytes 131104 | tf_op jit(solution)/shard_map/ppermute | solution.py:105
  17.5 0.0 copy-start
  17.5 0.7 %copy-done = bf16[256,512]{1,0:T(8,128)(2,1)} copy-done((bf16[256,512]{1,0:T(8,128)(2,1)}, bf16[256,512]{1,0:T(8,128)(2,1)S(1)}, u32[]{:S(2)}) %copy-start) | copy-done | bytes 262168
  18.2 2.5 %theirs.1 = f32[128,512]{1,0:T(8,128)} custom-call(s32[2,128]{1,0:T(2,128)} %bitcast.1, bf16[256,512]{1,0:T(8,128)(2,1)} %copy-done, bf16[512,512]{1,0:T(8,128)(2,1)} %get-tuple-element.8.refs_2_, bf16[512,512]{1,0:T(8,128)(2,1)} %get-tuple-element.9.refs_3_, f32[8,512]{1,0:T(8,128)} %get-tuple-element.10.refs_4_), custom_call_target="tpu_custom_call" | custom-call | tf_op jit(solution)/shard_map/theirs/pallas_call | solution.py:86
  20.8 1.5 %collective-permute-start.4 = (f32[128,512]{1,0:T(8,128)}, f32[128,512]{1,0:T(8,128)S(1)}, u32[]{:S(2)}, u32[]{:S(2)}) collective-permute-start(f32[128,512]{1,0:T(8,128)} %theirs.1), channel_id=1, source_target_pairs={{0,16},{16,0},{1,17},{17,1},{2,18},{18,2},{3,19},{19,3},{4,20},{20... | collective-permute-start | bytes 786440 | tf_op jit(solution)/shard_map/ppermute | solution.py:108
  22.3 2.6 %mine.1 = f32[128,512]{1,0:T(8,128)} custom-call(s32[2,128]{1,0:T(2,128)} %bitcast.2, bf16[256,512]{1,0:T(8,128)(2,1)} %copy-done, bf16[512,512]{1,0:T(8,128)(2,1)} %get-tuple-element.8.refs_2_, bf16[512,512]{1,0:T(8,128)(2,1)} %get-tuple-element.9.refs_3_, f32[8,512]{1,0:T(8,128)} %get-tuple-element.10.refs_4_), custom_call_target="tpu_custom_call" | custom-call | tf_op jit(solution)/shard_map/mine/pallas_call | solution.py:86
  24.8 4.5 %collective-permute-done.4 = f32[128,512]{1,0:T(8,128)S(1)} collective-permute-done((f32[128,512]{1,0:T(8,128)}, f32[128,512]{1,0:T(8,128)S(1)}, u32[]{:S(2)}, u32[]{:S(2)}) %collective-permute-start.4) | collective-permute-done | bytes 262176 | tf_op jit(solution)/shard_map/ppermute | solution.py:108
  29.3 1.7 %add.3 = f32[128,512]{1,0:T(8,128)} add(f32[128,512]{1,0:T(8,128)} %mine.1, f32[128,512]{1,0:T(8,128)S(1)} %collective-permute-done.4) | non-fusion elementwise | flops 65536 | bytes 786432 | tf_op jit(solution)/shard_map/add | solution.py:110
  (7 shorter events, 0.0 us)
Async XLA Ops:
  0.8 5.8 %collective-permute-start = (bf16[16,512]{1,0:T(8,128)(2,1)S(1)}, bf16[16,512]{1,0:T(8,128)(2,1)S(1)}, u32[]{:S(2)}, u32[]{:S(2)}) collective-permute-start(bf16[16,512]{1,0:T(8,128)(2,1)S(1)} %get-tuple-element.12), channel_id=1, source_target_pairs={{0,8},{1,9},{2,10},{3,11},{4,12},{5,13},{6,14},{7,15},{8,0},{9,1},... | collective-permute-start | bytes 49160 | tf_op jit(solution)/shard_map/ppermute | solution.py:105
  6.5 5.2 %collective-permute-start.1 = (bf16[32,512]{1,0:T(8,128)(2,1)S(1)}, bf16[32,512]{1,0:T(8,128)(2,1)S(1)}, u32[]{:S(2)}, u32[]{:S(2)}) collective-permute-start(bf16[32,512]{1,0:T(8,128)(2,1)S(1)} %pad_maximum_fusion.2), channel_id=1, source_target_pairs={{0,4},{1,5},{2,6},{3,7},{4,0},{5,1},{6,2},{7,3},{8,12},{9,13},{10,... | collective-permute-start | bytes 98312 | tf_op jit(solution)/shard_map/ppermute | solution.py:105
  11.8 4.3 %collective-permute-start.2 = (bf16[64,512]{1,0:T(8,128)(2,1)S(1)}, bf16[64,512]{1,0:T(8,128)(2,1)S(1)}, u32[]{:S(2)}, u32[]{:S(2)}) collective-permute-start(bf16[64,512]{1,0:T(8,128)(2,1)S(1)} %pad_maximum_fusion.1), channel_id=1, source_target_pairs={{0,2},{1,3},{2,0},{3,1},{4,6},{5,7},{6,4},{7,5},{8,10},{9,11},{10,... | collective-permute-start | bytes 196616 | tf_op jit(solution)/shard_map/ppermute | solution.py:105
  16.1 1.4 %collective-permute-start.3 = (bf16[128,512]{1,0:T(8,128)(2,1)S(1)}, bf16[128,512]{1,0:T(8,128)(2,1)S(1)}, u32[]{:S(2)}, u32[]{:S(2)}) collective-permute-start(bf16[128,512]{1,0:T(8,128)(2,1)S(1)} %pad_maximum_fusion), channel_id=1, source_target_pairs={{0,1},{1,0},{2,3},{3,2},{4,5},{5,4},{6,7},{7,6},{8,9},{9,8},{10,11... | collective-permute-start | bytes 393224 | tf_op jit(solution)/shard_map/ppermute | solution.py:105
  17.5 0.7 %copy-start = (bf16[256,512]{1,0:T(8,128)(2,1)}, bf16[256,512]{1,0:T(8,128)(2,1)S(1)}, u32[]{:S(2)}) copy-start(bf16[256,512]{1,0:T(8,128)(2,1)S(1)} %constant_dynamic-update-slice_fusion.refs_1_) | copy-start | bytes 786436
  20.8 8.6 %collective-permute-start.4 = (f32[128,512]{1,0:T(8,128)}, f32[128,512]{1,0:T(8,128)S(1)}, u32[]{:S(2)}, u32[]{:S(2)}) collective-permute-start(f32[128,512]{1,0:T(8,128)} %theirs.1), channel_id=1, source_target_pairs={{0,16},{16,0},{1,17},{17,1},{2,18},{18,2},{3,19},{19,3},{4,20},{20... | collective-permute-start | bytes 786440 | tf_op jit(solution)/shard_map/ppermute | solution.py:108

commit v2 on v1

v2 whole, which is shorter than its diff:
```python
import jax
import jax.numpy as jnp
from jax import lax
from jax.experimental import pallas as pl
from jax.experimental.pallas import tpu as pltpu
from jax.sharding import PartitionSpec as P

LANES = 128
PARTS = 2
CLOSE_BYTES = 1 << 19


def fits(array):
    return array.size * jnp.dtype(array.dtype).itemsize <= CLOSE_BYTES


def in_vmem(array):
    return pltpu.with_memory_space_constraint(array, pltpu.VMEM) if fits(array) else array


def result(shape, dtype):
    plain = jax.ShapeDtypeStruct(shape, dtype)
    return pltpu.VMEM(shape, dtype) if fits(plain) else plain


def decode_kernel(codes_ref, centroids_ref, high_ref, low_ref, norm_ref):
    spaces, width, centers = centroids_ref.shape
    count = codes_ref.shape[1]
    norm_ref[...] = jnp.zeros(norm_ref.shape, jnp.float32)

    def some_spaces(group, carry):
        for tile in range(count // LANES):
            lanes = pl.ds(tile * LANES, LANES)
            code_rows = codes_ref[pl.ds(pl.multiple_of(group * 8, 8), 8), lanes]
            squares = jnp.zeros((8, LANES), jnp.float32)
            for member in range(8):
                space = group * 8 + member
                codes = jnp.broadcast_to(code_rows[member : member + 1], (8, LANES))
                within = codes & (LANES - 1)
                part = codes >> (LANES.bit_length() - 1)
                pieces = []
                for row in range(0, width, 8):
                    value = None
                    for piece in range(centers // LANES):
                        table = centroids_ref[space, pl.ds(row, 8), pl.ds(piece * LANES, LANES)]
                        found = jnp.take_along_axis(table, within, axis=1)
                        value = found if piece == 0 else jnp.where(part == piece, found, value)
                    squares = squares + value * value
                    pieces.append(value)
                values = jnp.concatenate(pieces, axis=0)
                high = values.astype(jnp.bfloat16)
                rows = pl.ds(pl.multiple_of(space * width, width), width)
                high_ref[rows, lanes] = high
                low_ref[rows, lanes] = (values - high.astype(jnp.float32)).astype(jnp.bfloat16)
            norm_ref[:, lanes] += squares
        return carry

    lax.fori_loop(0, spaces // 8, some_spaces, 0)


def decode(part, code_ids, centroids):
    spaces, width, centers = centroids.shape
    spaces = spaces // PARTS
    count = code_ids.shape[1]
    whole = lambda *shape: pl.BlockSpec(shape, lambda i: (0,) * len(shape), memory_space=pltpu.VMEM)
    shapes = (
        result((spaces * width, count), jnp.bfloat16),
        result((spaces * width, count), jnp.bfloat16),
        result((8, count), jnp.float32),
    )
    return pl.pallas_call(
        decode_kernel,
        grid=(1,),
        in_specs=[
            pl.BlockSpec((spaces, count), lambda i: (part, 0)),
            pl.BlockSpec((spaces, width, centers), lambda i: (part, 0, 0)),
        ],
        out_specs=[whole(*shape.shape) for shape in shapes],
        out_shape=shapes,
        name="decode",
    )(code_ids, centroids)


def pick_kernel(own_rows, masks, order_ref, mine_ref, theirs_ref):
    half = lax.axis_index("sub")
    own = lax.axis_index("blk")
    place = lax.broadcasted_iota(jnp.int32, mine_ref.shape, 0)
    slot = place // own_rows
    holder = jnp.full(place.shape, own, jnp.int32)
    for bit, mask in enumerate(masks):
        holder = holder ^ (((slot >> bit) & 1) * mask)
    name = holder * own_rows + place % own_rows
    mine_ref[...] = jnp.where(name == order_ref[pl.ds(half, 1), :], 1.0, 0.0).astype(jnp.bfloat16)
    theirs_ref[...] = jnp.where(name == order_ref[pl.ds(1 - half, 1), :], 1.0, 0.0).astype(jnp.bfloat16)


def make_picks(own_rows, masks, order):
    shape = result((order.size, order.shape[1]), jnp.bfloat16)
    return pl.pallas_call(
        lambda *refs: pick_kernel(own_rows, masks, *refs),
        out_shape=(shape, shape),
        name="picks",
    )(order)


def distance_kernel(pick_ref, queries_ref, *refs):
    out_ref = refs[-1]
    picked = lax.dot_general(
        pick_ref[...], queries_ref[...], (((0,), (0,)), ((), ())), preferred_element_type=jnp.float32
    )
    total = jnp.sum(picked * picked, axis=1, keepdims=True)
    for part in range(PARTS):
        total = total + jnp.sum(refs[3 * part + 2][...], axis=0, keepdims=True)
    left = (picked * -2.0).astype(jnp.bfloat16)
    for part in range(PARTS):
        high_ref, low_ref, _ = refs[3 * part : 3 * part + 3]
        columns = high_ref.shape[0]
        piece = left[:, part * columns : (part + 1) * columns]
        total = total + jnp.dot(piece, high_ref[...], preferred_element_type=jnp.float32)
        total = total + jnp.dot(piece, low_ref[...], preferred_element_type=jnp.float32)
    out_ref[...] = total


def distances_of(pick, queries, vectors):
    return pl.pallas_call(
        distance_kernel, out_shape=result((pick.shape[1], vectors[0].shape[1]), jnp.float32)
    )(*[in_vmem(array) for array in (pick, queries, *vectors)])


def solution(mesh):
    blocks = mesh.shape["blk"]
    halves = mesh.shape["sub"]
    masks = []
    while (1 << len(masks)) < blocks:
        masks.append((blocks >> (len(masks) + 1)) | 1)

    def local(queries, centroids, code_ids, query_order):
        own_rows = queries.shape[0]
        rows = queries.astype(jnp.bfloat16)
        for mask in masks:
            arrived = lax.ppermute(rows, "blk", [(i, i ^ mask) for i in range(blocks)])
            rows = jnp.concatenate([rows, arrived], axis=0)
        pick_mine, pick_theirs = make_picks(own_rows, masks, query_order.reshape(halves, -1))
        vectors = []
        for part in range(PARTS):
            vectors.extend(decode(part, code_ids, centroids))
        theirs = distances_of(pick_theirs, rows, vectors)
        arrived = lax.ppermute(theirs, "sub", [(i, i ^ 1) for i in range(halves)])
        mine = distances_of(pick_mine, rows, vectors)
        return mine + arrived

    in_specs = (P("blk", "sub"), P("sub", None, None), P("sub", "blk"), P())
    return jax.shard_map(local, mesh=mesh, in_specs=in_specs, out_specs=P("sub", "blk"), check_vma=False)
```

time: 31.3 us -> 27 us (0.86)
  Pallas kernels: 8.38 us -> 4.88 us
  waiting for transfers between devices: 10.3 us -> 11.3 us
  other arithmetic: 2.47 us -> 1.52 us
  local copies, waits for them, and re-layouts: 0.72 us -> 0.02 us
    pallas_call x3 -> x5, Pallas kernels: 8.38 us -> 4.88 us  [the longest x2 3.17 us: decode(): pl.pallas_call(decode_kernel, grid=(1,), in_specs=[pl.BlockSpec((spaces,...]
    ppermute x1, waiting for transfers between devices: 4.5 us -> 6.6 us  [local(): arrived = lax.ppermute(theirs, 'sub', [(i, i ^ 1) for i in range(halves)])]
    ppermute x4, waiting for transfers between devices: 5.8 us -> 4.74 us  [local(): arrived = lax.ppermute(rows, 'blk', [(i, i ^ mask) for i in range(blocks)])]
    add x1, other arithmetic: 1.69 us -> 0.74 us  [local(): return mine + arrived]
    unnamed x5 -> x3, local copies, waits for them, and re-layouts: 0.71 us -> 0.01 us
  transfers between devices with their start and end apart: 5 -> 5, of which waited for: 4 -> 4; matrix products, arithmetic and copies ran while one was open for 0% -> 0% of each run, Pallas kernels for 19% -> 16%
where the time goes in v2:
time: 27 us; the launch traced here: 26.8 us
  waiting for transfers between devices  11.3 us (42%)
  starting transfers between devices  8.99 us (33%)
  Pallas kernels  4.88 us (18%)
  other arithmetic  1.52 us (6%)
    ppermute x4, starting transfers between devices, local(): arrived = lax.ppermute(rows, 'blk', [(i, i ^ mask) for i in range(blocks)])  7.41 us
    ppermute x1, waiting for transfers between devices, local(): arrived = lax.ppermute(theirs, 'sub', [(i, i ^ 1) for i in range(halves)])  6.6 us
    ppermute x4, waiting for transfers between devices, local(): arrived = lax.ppermute(rows, 'blk', [(i, i ^ mask) for i in range(blocks)])  4.74 us
    pallas_call x2, Pallas kernels, decode(): pl.pallas_call(decode_kernel, grid=(1,), in_specs=[pl.BlockSpec((spaces,...  3.17 us
    ppermute x1, starting transfers between devices, local(): arrived = lax.ppermute(theirs, 'sub', [(i, i ^ 1) for i in range(halves)])  1.58 us
    pallas_call x2, Pallas kernels, distances_of(): pl.pallas_call(distance_kernel, out_shape=result((pick.shape[1], vectors[...  0.92 us
    pallas_call x1, Pallas kernels, make_picks(): pl.pallas_call(lambda *refs: pick_kernel(own_rows, masks, *refs), out_sha...  0.79 us
    unnamed x1, other arithmetic  0.76 us
  transfers between devices with their start and end apart: 5, of which 4 were waited for; matrix products, arithmetic and copies ran while one was open for 0% of the time, Pallas kernels for 16%

profile of v2, /device:TPU:0, one launch (start us, length us, event | category | flops | bytes accessed | tf_op | source)
XLA Modules:
  0.0 26.8 jit_solution(3055002540965222228)
XLA Ops:
  0.0 0.8 %constant_dynamic-update-slice_fusion.4 = (bf16[256,512]{1,0:T(8,128)(2,1)S(1)}, bf16[16,512]{1,0:T(8,128)(2,1)S(1)}) fusion(f32[16,512]{1,0:T(8,128)} %param.4), kind=kLoop, calls=%fused_computation.7 | loop fusion | flops 8191 | bytes 65536
  0.8 3.5 %collective-permute-start = (bf16[16,512]{1,0:T(8,128)(2,1)S(1)}, bf16[16,512]{1,0:T(8,128)(2,1)S(1)}, u32[]{:S(2)}, u32[]{:S(2)}) collective-permute-start(bf16[16,512]{1,0:T(8,128)(2,1)S(1)} %get-tuple-element.22), channel_id=1, source_target_pairs={{0,9},{1,8},{2,11},{3,10},{4,13},{5,12},{6,15},{7,14},{8,1},{9,0},... | collective-permute-start | bytes 49160 | tf_op jit(solution)/shard_map/ppermute | solution.py:141
  4.3 1.4 %collective-permute-done = bf16[16,512]{1,0:T(8,128)(2,1)S(1)} collective-permute-done((bf16[16,512]{1,0:T(8,128)(2,1)S(1)}, bf16[16,512]{1,0:T(8,128)(2,1)S(1)}, u32[]{:S(2)}, u32[]{:S(2)}) %collective-permute-start) | collective-permute-done | bytes 16416 | tf_op jit(solution)/shard_map/ppermute | solution.py:141
  5.7 1.9 %collective-permute-start.1 = (bf16[32,512]{1,0:T(8,128)(2,1)S(1)}, bf16[32,512]{1,0:T(8,128)(2,1)S(1)}, u32[]{:S(2)}, u32[]{:S(2)}) collective-permute-start(bf16[32,512]{1,0:T(8,128)(2,1)S(1)} %pad_maximum_fusion.2), channel_id=1, source_target_pairs={{0,5},{1,4},{2,7},{3,6},{4,1},{5,0},{6,3},{7,2},{8,13},{9,12},{10,... | collective-permute-start | bytes 98312 | tf_op jit(solution)/shard_map/ppermute | solution.py:141
  7.6 1.6 %decode.3 = (bf16[256,512]{1,0:T(8,128)(2,1)S(1)}, bf16[256,512]{1,0:T(8,128)(2,1)S(1)}, f32[8,512]{1,0:T(8,128)S(1)}) custom-call(s32[32,512]{1,0:T(8,128)} %codes_ref.3, f32[32,16,256]{2,1,0:T(8,128)} %centroids_ref.3), custom_call_target="tpu_custom_call" | custom-call | tf_op jit(solution)/shard_map/decode/pallas_call | solution.py:71
  9.2 1.6 %decode.2 = (bf16[256,512]{1,0:T(8,128)(2,1)S(1)}, bf16[256,512]{1,0:T(8,128)(2,1)S(1)}, f32[8,512]{1,0:T(8,128)S(1)}) custom-call(s32[32,512]{1,0:T(8,128)} %codes_ref.3, f32[32,16,256]{2,1,0:T(8,128)} %centroids_ref.3), custom_call_target="tpu_custom_call" | custom-call | tf_op jit(solution)/shard_map/decode/pallas_call | solution.py:71
  10.8 0.8 %picks.1 = (bf16[256,128]{1,0:T(8,128)(2,1)S(1)}, bf16[256,128]{1,0:T(8,128)(2,1)S(1)}) custom-call(s32[2,128]{1,0:T(2,128)} %bitcast.1), custom_call_target="tpu_custom_call" | custom-call | tf_op jit(solution)/shard_map/picks/pallas_call | solution.py:99
  11.6 0.0 collective-permute-done.1
  11.6 1.6 %collective-permute-start.2 = (bf16[64,512]{1,0:T(8,128)(2,1)S(1)}, bf16[64,512]{1,0:T(8,128)(2,1)S(1)}, u32[]{:S(2)}, u32[]{:S(2)}) collective-permute-start(bf16[64,512]{1,0:T(8,128)(2,1)S(1)} %pad_maximum_fusion.1), channel_id=1, source_target_pairs={{0,3},{1,2},{2,1},{3,0},{4,7},{5,6},{6,5},{7,4},{8,11},{9,10},{10,... | collective-permute-start | bytes 196616 | tf_op jit(solution)/shard_map/ppermute | solution.py:141
  13.2 2.3 %collective-permute-done.2 = bf16[64,512]{1,0:T(8,128)(2,1)S(1)} collective-permute-done((bf16[64,512]{1,0:T(8,128)(2,1)S(1)}, bf16[64,512]{1,0:T(8,128)(2,1)S(1)}, u32[]{:S(2)}, u32[]{:S(2)}) %collective-permute-start.2) | collective-permute-done | bytes 65568 | tf_op jit(solution)/shard_map/ppermute | solution.py:141
  15.5 0.5 %collective-permute-start.3 = (bf16[128,512]{1,0:T(8,128)(2,1)S(1)}, bf16[128,512]{1,0:T(8,128)(2,1)S(1)}, u32[]{:S(2)}, u32[]{:S(2)}) collective-permute-start(bf16[128,512]{1,0:T(8,128)(2,1)S(1)} %pad_maximum_fusion), channel_id=1, source_target_pairs={{0,1},{1,0},{2,3},{3,2},{4,5},{5,4},{6,7},{7,6},{8,9},{9,8},{10,11... | collective-permute-start | bytes 393224 | tf_op jit(solution)/shard_map/ppermute | solution.py:141
  16.0 1.0 %collective-permute-done.3 = bf16[128,512]{1,0:T(8,128)(2,1)S(1)} collective-permute-done((bf16[128,512]{1,0:T(8,128)(2,1)S(1)}, bf16[128,512]{1,0:T(8,128)(2,1)S(1)}, u32[]{:S(2)}, u32[]{:S(2)}) %collective-permute-start.3) | collective-permute-done | bytes 131104 | tf_op jit(solution)/shard_map/ppermute | solution.py:141
  17.0 0.5 %shard_map.47 = f32[128,512]{1,0:T(8,128)S(1)} custom-call(bf16[256,128]{1,0:T(8,128)(2,1)S(1)} %get-tuple-element.20.pick_ref, bf16[256,512]{1,0:T(8,128)(2,1)S(1)} %constant_dynamic-update-slice_fusion.queries_ref, bf16[256,512]{1,0:T(8,128)(2,1)S(1)} %get-tuple-element.14.refs_0_, bf16[256,512]{1,0:T(8,128)(2,1)S(1)} %get-tuple-element.15.refs_1_, ...), custom_call_target="tpu_custom_call" | custom-call | tf_op jit(solution)/shard_map/pallas_call | solution.py:125
  17.4 1.6 %collective-permute-start.4 = (f32[128,512]{1,0:T(8,128)S(1)}, f32[128,512]{1,0:T(8,128)S(1)}, u32[]{:S(2)}, u32[]{:S(2)}) collective-permute-start(f32[128,512]{1,0:T(8,128)S(1)} %shard_map.47), channel_id=1, source_target_pairs={{0,16},{16,0},{1,17},{17,1},{2,18},{18,2},{3,19},{19,3},{4,20},{20... | collective-permute-start | bytes 786440 | tf_op jit(solution)/shard_map/ppermute | solution.py:148
  19.0 0.5 %shard_map.46 = f32[128,512]{1,0:T(8,128)S(1)} custom-call(bf16[256,128]{1,0:T(8,128)(2,1)S(1)} %get-tuple-element.13.pick_ref, bf16[256,512]{1,0:T(8,128)(2,1)S(1)} %constant_dynamic-update-slice_fusion.queries_ref, bf16[256,512]{1,0:T(8,128)(2,1)S(1)} %get-tuple-element.14.refs_0_, bf16[256,512]{1,0:T(8,128)(2,1)S(1)} %get-tuple-element.15.refs_1_, ...), custom_call_target="tpu_custom_call" | custom-call | tf_op jit(solution)/shard_map/pallas_call | solution.py:125
  19.5 6.6 %collective-permute-done.4 = f32[128,512]{1,0:T(8,128)S(1)} collective-permute-done((f32[128,512]{1,0:T(8,128)S(1)}, f32[128,512]{1,0:T(8,128)S(1)}, u32[]{:S(2)}, u32[]{:S(2)}) %collective-permute-start.4) | collective-permute-done | bytes 262176 | tf_op jit(solution)/shard_map/ppermute | solution.py:148
  26.1 0.7 %add.3 = f32[128,512]{1,0:T(8,128)} add(f32[128,512]{1,0:T(8,128)S(1)} %shard_map.46, f32[128,512]{1,0:T(8,128)S(1)} %collective-permute-done.4) | non-fusion elementwise | flops 65536 | bytes 786432 | tf_op jit(solution)/shard_map/add | solution.py:150
  (7 shorter events, 0.0 us)
Async XLA Ops:
  0.8 4.9 %collective-permute-start = (bf16[16,512]{1,0:T(8,128)(2,1)S(1)}, bf16[16,512]{1,0:T(8,128)(2,1)S(1)}, u32[]{:S(2)}, u32[]{:S(2)}) collective-permute-start(bf16[16,512]{1,0:T(8,128)(2,1)S(1)} %get-tuple-element.22), channel_id=1, source_target_pairs={{0,9},{1,8},{2,11},{3,10},{4,13},{5,12},{6,15},{7,14},{8,1},{9,0},... | collective-permute-start | bytes 49160 | tf_op jit(solution)/shard_map/ppermute | solution.py:141
  5.7 5.9 %collective-permute-start.1 = (bf16[32,512]{1,0:T(8,128)(2,1)S(1)}, bf16[32,512]{1,0:T(8,128)(2,1)S(1)}, u32[]{:S(2)}, u32[]{:S(2)}) collective-permute-start(bf16[32,512]{1,0:T(8,128)(2,1)S(1)} %pad_maximum_fusion.2), channel_id=1, source_target_pairs={{0,5},{1,4},{2,7},{3,6},{4,1},{5,0},{6,3},{7,2},{8,13},{9,12},{10,... | collective-permute-start | bytes 98312 | tf_op jit(solution)/shard_map/ppermute | solution.py:141
  11.6 3.9 %collective-permute-start.2 = (bf16[64,512]{1,0:T(8,128)(2,1)S(1)}, bf16[64,512]{1,0:T(8,128)(2,1)S(1)}, u32[]{:S(2)}, u32[]{:S(2)}) collective-permute-start(bf16[64,512]{1,0:T(8,128)(2,1)S(1)} %pad_maximum_fusion.1), channel_id=1, source_target_pairs={{0,3},{1,2},{2,1},{3,0},{4,7},{5,6},{6,5},{7,4},{8,11},{9,10},{10,... | collective-permute-start | bytes 196616 | tf_op jit(solution)/shard_map/ppermute | solution.py:141
  15.5 1.4 %collective-permute-start.3 = (bf16[128,512]{1,0:T(8,128)(2,1)S(1)}, bf16[128,512]{1,0:T(8,128)(2,1)S(1)}, u32[]{:S(2)}, u32[]{:S(2)}) collective-permute-start(bf16[128,512]{1,0:T(8,128)(2,1)S(1)} %pad_maximum_fusion), channel_id=1, source_target_pairs={{0,1},{1,0},{2,3},{3,2},{4,5},{5,4},{6,7},{7,6},{8,9},{9,8},{10,11... | collective-permute-start | bytes 393224 | tf_op jit(solution)/shard_map/ppermute | solution.py:141
  17.4 8.6 %collective-permute-start.4 = (f32[128,512]{1,0:T(8,128)S(1)}, f32[128,512]{1,0:T(8,128)S(1)}, u32[]{:S(2)}, u32[]{:S(2)}) collective-permute-start(f32[128,512]{1,0:T(8,128)S(1)} %shard_map.47), channel_id=1, source_target_pairs={{0,16},{16,0},{1,17},{17,1},{2,18},{18,2},{3,19},{19,3},{4,20},{20... | collective-permute-start | bytes 786440 | tf_op jit(solution)/shard_map/ppermute | solution.py:148

commit v3 on v2

--- a/solution.py
+++ b/solution.py
@@ -7,6 +7,7 @@
 
 LANES = 128
 PARTS = 2
+LEVEL = 32768.0
 CLOSE_BYTES = 1 << 19
 
 
@@ -104,26 +105,33 @@
 
 
 def distance_kernel(pick_ref, queries_ref, *refs):
-    out_ref = refs[-1]
+    vector_refs, out_refs = refs[: 3 * PARTS], refs[3 * PARTS :]
     picked = lax.dot_general(
         pick_ref[...], queries_ref[...], (((0,), (0,)), ((), ())), preferred_element_type=jnp.float32
     )
     total = jnp.sum(picked * picked, axis=1, keepdims=True)
     for part in range(PARTS):
-        total = total + jnp.sum(refs[3 * part + 2][...], axis=0, keepdims=True)
+        total = total + jnp.sum(vector_refs[3 * part + 2][...], axis=0, keepdims=True)
     left = (picked * -2.0).astype(jnp.bfloat16)
     for part in range(PARTS):
-        high_ref, low_ref, _ = refs[3 * part : 3 * part + 3]
+        high_ref, low_ref, _ = vector_refs[3 * part : 3 * part + 3]
         columns = high_ref.shape[0]
         piece = left[:, part * columns : (part + 1) * columns]
         total = total + jnp.dot(piece, high_ref[...], preferred_element_type=jnp.float32)
         total = total + jnp.dot(piece, low_ref[...], preferred_element_type=jnp.float32)
-    out_ref[...] = total
+    if len(out_refs) == 2:
+        largest = jnp.maximum(jnp.max(jnp.abs(total)), 1e-30)
+        total = total * (LEVEL / largest)
+        out_refs[1][...] = jnp.full(out_refs[1].shape, largest * (1.0 / LEVEL), jnp.float32)
+    out_refs[0][...] = total
 
 
-def distances_of(pick, queries, vectors):
+def distances_of(pick, queries, vectors, scaled):
+    shapes = (result((pick.shape[1], vectors[0].shape[1]), jnp.float32),)
+    if scaled:
+        shapes += (result((8, shapes[0].shape[1]), jnp.float32),)
     return pl.pallas_call(
-        distance_kernel, out_shape=result((pick.shape[1], vectors[0].shape[1]), jnp.float32)
+        distance_kernel, out_shape=shapes
     )(*[in_vmem(array) for array in (pick, queries, *vectors)])
 
 
@@ -144,10 +152,13 @@
         vectors = []
         for part in range(PARTS):
             vectors.extend(decode(part, code_ids, centroids))
-        theirs = distances_of(pick_theirs, rows, vectors)
-        arrived = lax.ppermute(theirs, "sub", [(i, i ^ 1) for i in range(halves)])
-        mine = distances_of(pick_mine, rows, vectors)
-        return mine + arrived
+        theirs, scale = distances_of(pick_theirs, rows, vectors, True)
+        swap = [(i, i ^ 1) for i in range(halves)]
+        arrived = lax.ppermute(theirs.astype(jnp.float16), "sub", swap)
+        scale = lax.ppermute(scale, "sub", swap)
+        (mine,) = distances_of(pick_mine, rows, vectors, False)
+        arrived = arrived.astype(jnp.float32).reshape(-1, *scale.shape) * scale
+        return mine + arrived.reshape(mine.shape)
 
     in_specs = (P("blk", "sub"), P("sub", None, None), P("sub", "blk"), P())
     return jax.shard_map(local, mesh=mesh, in_specs=in_specs, out_specs=P("sub", "blk"), check_vma=False)

time: 27 us -> 24.8 us (0.919)
  waiting for transfers between devices: 11.3 us -> 8.36 us
  starting transfers between devices: 8.99 us -> 9.5 us
    ppermute x1 -> x2, waiting for transfers between devices: 6.6 us -> 3.62 us  [the longest x1 3.61 us: local(): scale = lax.ppermute(scale, 'sub', swap)]
    ppermute x1 -> x2, starting transfers between devices: 1.58 us -> 2.09 us  [the longest x1 1.58 us: local(): arrived = lax.ppermute(theirs.astype(jnp.float16), 'sub', swap)]
  transfers between devices with their start and end apart: 5 -> 6, of which waited for: 4 -> 4; matrix products, arithmetic and copies ran while one was open for 0% -> 0% of each run, Pallas kernels for 16% -> 18%
where the time goes in v3:
time: 24.8 us; the launch traced here: 24.5 us
  starting transfers between devices  9.5 us (38%)
  waiting for transfers between devices  8.36 us (34%)
  Pallas kernels  5.06 us (20%)
  other arithmetic  1.54 us (6%)
    ppermute x4, starting transfers between devices, local(): arrived = lax.ppermute(rows, 'blk', [(i, i ^ mask) for i in range(blocks)])  7.41 us
    ppermute x4, waiting for transfers between devices, local(): arrived = lax.ppermute(rows, 'blk', [(i, i ^ mask) for i in range(blocks)])  4.74 us
    ppermute x1, waiting for transfers between devices, local(): scale = lax.ppermute(scale, 'sub', swap)  3.61 us
    pallas_call x2, Pallas kernels, decode(): pl.pallas_call(decode_kernel, grid=(1,), in_specs=[pl.BlockSpec((spaces,...  3.17 us
    ppermute x1, starting transfers between devices, local(): arrived = lax.ppermute(theirs.astype(jnp.float16), 'sub', swap)  1.58 us
    pallas_call x2, Pallas kernels, distances_of(): pl.pallas_call(distance_kernel, out_shape=shapes)  1.1 us
    pallas_call x1, Pallas kernels, make_picks(): pl.pallas_call(lambda *refs: pick_kernel(own_rows, masks, *refs), out_sha...  0.79 us
    unnamed x1, other arithmetic  0.76 us
  transfers between devices with their start and end apart: 6, of which 4 were waited for; matrix products, arithmetic and copies ran while one was open for 0% of the time, Pallas kernels for 18%

profile of v3, /device:TPU:0, one launch (start us, length us, event | category | flops | bytes accessed | tf_op | source)
XLA Modules:
  0.0 24.5 jit_solution(2817904302229260397)
XLA Ops:
  0.0 0.8 %constant_dynamic-update-slice_fusion.4 = (bf16[256,512]{1,0:T(8,128)(2,1)S(1)}, bf16[16,512]{1,0:T(8,128)(2,1)S(1)}) fusion(f32[16,512]{1,0:T(8,128)} %param.4), kind=kLoop, calls=%fused_computation.9 | loop fusion | flops 8191 | bytes 65536
  0.8 3.5 %collective-permute-start = (bf16[16,512]{1,0:T(8,128)(2,1)S(1)}, bf16[16,512]{1,0:T(8,128)(2,1)S(1)}, u32[]{:S(2)}, u32[]{:S(2)}) collective-permute-start(bf16[16,512]{1,0:T(8,128)(2,1)S(1)} %get-tuple-element.26), channel_id=1, source_target_pairs={{0,9},{1,8},{2,11},{3,10},{4,13},{5,12},{6,15},{7,14},{8,1},{9,0},... | collective-permute-start | bytes 49160 | tf_op jit(solution)/shard_map/ppermute | solution.py:149
  4.3 1.4 %collective-permute-done = bf16[16,512]{1,0:T(8,128)(2,1)S(1)} collective-permute-done((bf16[16,512]{1,0:T(8,128)(2,1)S(1)}, bf16[16,512]{1,0:T(8,128)(2,1)S(1)}, u32[]{:S(2)}, u32[]{:S(2)}) %collective-permute-start) | collective-permute-done | bytes 16416 | tf_op jit(solution)/shard_map/ppermute | solution.py:149
  5.7 1.9 %collective-permute-start.1 = (bf16[32,512]{1,0:T(8,128)(2,1)S(1)}, bf16[32,512]{1,0:T(8,128)(2,1)S(1)}, u32[]{:S(2)}, u32[]{:S(2)}) collective-permute-start(bf16[32,512]{1,0:T(8,128)(2,1)S(1)} %pad_maximum_fusion.2), channel_id=1, source_target_pairs={{0,5},{1,4},{2,7},{3,6},{4,1},{5,0},{6,3},{7,2},{8,13},{9,12},{10,... | collective-permute-start | bytes 98312 | tf_op jit(solution)/shard_map/ppermute | solution.py:149
  7.6 1.6 %decode.2 = (bf16[256,512]{1,0:T(8,128)(2,1)S(1)}, bf16[256,512]{1,0:T(8,128)(2,1)S(1)}, f32[8,512]{1,0:T(8,128)S(1)}) custom-call(s32[32,512]{1,0:T(8,128)} %codes_ref.3, f32[32,16,256]{2,1,0:T(8,128)} %centroids_ref.3), custom_call_target="tpu_custom_call" | custom-call | tf_op jit(solution)/shard_map/decode/pallas_call | solution.py:72
  9.2 1.6 %decode.3 = (bf16[256,512]{1,0:T(8,128)(2,1)S(1)}, bf16[256,512]{1,0:T(8,128)(2,1)S(1)}, f32[8,512]{1,0:T(8,128)S(1)}) custom-call(s32[32,512]{1,0:T(8,128)} %codes_ref.3, f32[32,16,256]{2,1,0:T(8,128)} %centroids_ref.3), custom_call_target="tpu_custom_call" | custom-call | tf_op jit(solution)/shard_map/decode/pallas_call | solution.py:72
  10.8 0.8 %picks.1 = (bf16[256,128]{1,0:T(8,128)(2,1)S(1)}, bf16[256,128]{1,0:T(8,128)(2,1)S(1)}) custom-call(s32[2,128]{1,0:T(2,128)} %bitcast.5), custom_call_target="tpu_custom_call" | custom-call | tf_op jit(solution)/shard_map/picks/pallas_call | solution.py:100
  11.6 0.0 collective-permute-done.1
  11.6 1.6 %collective-permute-start.2 = (bf16[64,512]{1,0:T(8,128)(2,1)S(1)}, bf16[64,512]{1,0:T(8,128)(2,1)S(1)}, u32[]{:S(2)}, u32[]{:S(2)}) collective-permute-start(bf16[64,512]{1,0:T(8,128)(2,1)S(1)} %pad_maximum_fusion.1), channel_id=1, source_target_pairs={{0,3},{1,2},{2,1},{3,0},{4,7},{5,6},{6,5},{7,4},{8,11},{9,10},{10,... | collective-permute-start | bytes 196616 | tf_op jit(solution)/shard_map/ppermute | solution.py:149
  13.2 2.3 %collective-permute-done.2 = bf16[64,512]{1,0:T(8,128)(2,1)S(1)} collective-permute-done((bf16[64,512]{1,0:T(8,128)(2,1)S(1)}, bf16[64,512]{1,0:T(8,128)(2,1)S(1)}, u32[]{:S(2)}, u32[]{:S(2)}) %collective-permute-start.2) | collective-permute-done | bytes 65568 | tf_op jit(solution)/shard_map/ppermute | solution.py:149
  15.5 0.5 %collective-permute-start.3 = (bf16[128,512]{1,0:T(8,128)(2,1)S(1)}, bf16[128,512]{1,0:T(8,128)(2,1)S(1)}, u32[]{:S(2)}, u32[]{:S(2)}) collective-permute-start(bf16[128,512]{1,0:T(8,128)(2,1)S(1)} %pad_maximum_fusion), channel_id=1, source_target_pairs={{0,1},{1,0},{2,3},{3,2},{4,5},{5,4},{6,7},{7,6},{8,9},{9,8},{10,11... | collective-permute-start | bytes 393224 | tf_op jit(solution)/shard_map/ppermute | solution.py:149
  16.0 1.0 %collective-permute-done.3 = bf16[128,512]{1,0:T(8,128)(2,1)S(1)} collective-permute-done((bf16[128,512]{1,0:T(8,128)(2,1)S(1)}, bf16[128,512]{1,0:T(8,128)(2,1)S(1)}, u32[]{:S(2)}, u32[]{:S(2)}) %collective-permute-start.3) | collective-permute-done | bytes 131104 | tf_op jit(solution)/shard_map/ppermute | solution.py:149
  17.0 0.6 %shard_map.47 = (f32[128,512]{1,0:T(8,128)S(1)}, f32[8,512]{1,0:T(8,128)S(1)}) custom-call(bf16[256,128]{1,0:T(8,128)(2,1)S(1)} %get-tuple-element.22.pick_ref, bf16[256,512]{1,0:T(8,128)(2,1)S(1)} %constant_dynamic-update-slice_fusion.queries_ref, bf16[256,512]{1,0:T(8,128)(2,1)S(1)} %get-tuple-element.16.refs_0_, ...), custom_call_target="tpu_custom_call" | custom-call | tf_op jit(solution)/shard_map/pallas_call | solution.py:133
  17.6 1.6 %collective-permute-start.4 = (f16[128,512]{1,0:T(8,128)(2,1)S(1)}, f16[128,512]{1,0:T(8,128)(2,1)S(1)}, u32[]{:S(2)}, u32[]{:S(2)}) collective-permute-start(f16[128,512]{1,0:T(8,128)(2,1)S(1)} %convert_element_type.10), channel_id=1, source_target_pairs={{0,16},{16,0},{1,17},{17,1},{2,18},{18,2},{3,19},{19,3},{4,20},{20... | collective-permute-start | bytes 393224 | tf_op jit(solution)/shard_map/ppermute | solution.py:157
  19.2 0.5 %collective-permute-start.5 = (f32[8,512]{1,0:T(8,128)S(1)}, f32[8,512]{1,0:T(8,128)S(1)}, u32[]{:S(2)}, u32[]{:S(2)}) collective-permute-start(f32[8,512]{1,0:T(8,128)S(1)} %get-tuple-element.24), channel_id=1, source_target_pairs={{0,16},{16,0},{1,17},{17,1},{2,18},{18,2},{3,19},{19,3},{4,20},{20... | collective-permute-start | bytes 49160 | tf_op jit(solution)/shard_map/ppermute | solution.py:158
  19.7 0.5 %shard_map.46 = f32[128,512]{1,0:T(8,128)S(1)} custom-call(bf16[256,128]{1,0:T(8,128)(2,1)S(1)} %get-tuple-element.15.pick_ref, bf16[256,512]{1,0:T(8,128)(2,1)S(1)} %constant_dynamic-update-slice_fusion.queries_ref, bf16[256,512]{1,0:T(8,128)(2,1)S(1)} %get-tuple-element.16.refs_0_, bf16[256,512]{1,0:T(8,128)(2,1)S(1)} %get-tuple-element.17.refs_1_, ...), custom_call_target="tpu_custom_call" | custom-call | tf_op jit(solution)/shard_map/pallas_call | solution.py:133
  20.2 3.6 %collective-permute-done.5 = f32[8,512]{1,0:T(8,128)S(1)} collective-permute-done((f32[8,512]{1,0:T(8,128)S(1)}, f32[8,512]{1,0:T(8,128)S(1)}, u32[]{:S(2)}, u32[]{:S(2)}) %collective-permute-start.5) | collective-permute-done | bytes 16416 | tf_op jit(solution)/shard_map/ppermute | solution.py:158
  23.8 0.0 collective-permute-done.4
  23.8 0.7 %fusion = f32[128,512]{1,0:T(8,128)} fusion(f32[128,512]{1,0:T(8,128)S(1)} %shard_map.46, f16[128,512]{1,0:T(8,128)(2,1)S(1)} %collective-permute-done.4, f32[8,512]{1,0:T(8,128)S(1)} %collective-permute-done.5), kind=kLoop, calls=%fused_computation.1 | loop fusion | flops 196608 | bytes 671744 | tf_op jit(solution)/shard_map/add | solution.py:161
  (8 shorter events, 0.1 us)
Async XLA Ops:
  0.8 4.9 %collective-permute-start = (bf16[16,512]{1,0:T(8,128)(2,1)S(1)}, bf16[16,512]{1,0:T(8,128)(2,1)S(1)}, u32[]{:S(2)}, u32[]{:S(2)}) collective-permute-start(bf16[16,512]{1,0:T(8,128)(2,1)S(1)} %get-tuple-element.26), channel_id=1, source_target_pairs={{0,9},{1,8},{2,11},{3,10},{4,13},{5,12},{6,15},{7,14},{8,1},{9,0},... | collective-permute-start | bytes 49160 | tf_op jit(solution)/shard_map/ppermute | solution.py:149
  5.7 5.9 %collective-permute-start.1 = (bf16[32,512]{1,0:T(8,128)(2,1)S(1)}, bf16[32,512]{1,0:T(8,128)(2,1)S(1)}, u32[]{:S(2)}, u32[]{:S(2)}) collective-permute-start(bf16[32,512]{1,0:T(8,128)(2,1)S(1)} %pad_maximum_fusion.2), channel_id=1, source_target_pairs={{0,5},{1,4},{2,7},{3,6},{4,1},{5,0},{6,3},{7,2},{8,13},{9,12},{10,... | collective-permute-start | bytes 98312 | tf_op jit(solution)/shard_map/ppermute | solution.py:149
  11.6 3.9 %collective-permute-start.2 = (bf16[64,512]{1,0:T(8,128)(2,1)S(1)}, bf16[64,512]{1,0:T(8,128)(2,1)S(1)}, u32[]{:S(2)}, u32[]{:S(2)}) collective-permute-start(bf16[64,512]{1,0:T(8,128)(2,1)S(1)} %pad_maximum_fusion.1), channel_id=1, source_target_pairs={{0,3},{1,2},{2,1},{3,0},{4,7},{5,6},{6,5},{7,4},{8,11},{9,10},{10,... | collective-permute-start | bytes 196616 | tf_op jit(solution)/shard_map/ppermute | solution.py:149
  15.5 1.4 %collective-permute-start.3 = (bf16[128,512]{1,0:T(8,128)(2,1)S(1)}, bf16[128,512]{1,0:T(8,128)(2,1)S(1)}, u32[]{:S(2)}, u32[]{:S(2)}) collective-permute-start(bf16[128,512]{1,0:T(8,128)(2,1)S(1)} %pad_maximum_fusion), channel_id=1, source_target_pairs={{0,1},{1,0},{2,3},{3,2},{4,5},{5,4},{6,7},{7,6},{8,9},{9,8},{10,11... | collective-permute-start | bytes 393224 | tf_op jit(solution)/shard_map/ppermute | solution.py:149
  17.6 6.2 %collective-permute-start.4 = (f16[128,512]{1,0:T(8,128)(2,1)S(1)}, f16[128,512]{1,0:T(8,128)(2,1)S(1)}, u32[]{:S(2)}, u32[]{:S(2)}) collective-permute-start(f16[128,512]{1,0:T(8,128)(2,1)S(1)} %convert_element_type.10), channel_id=1, source_target_pairs={{0,16},{16,0},{1,17},{17,1},{2,18},{18,2},{3,19},{19,3},{4,20},{20... | collective-permute-start | bytes 393224 | tf_op jit(solution)/shard_map/ppermute | solution.py:157
  19.2 4.6 %collective-permute-start.5 = (f32[8,512]{1,0:T(8,128)S(1)}, f32[8,512]{1,0:T(8,128)S(1)}, u32[]{:S(2)}, u32[]{:S(2)}) collective-permute-start(f32[8,512]{1,0:T(8,128)S(1)} %get-tuple-element.24), channel_id=1, source_target_pairs={{0,16},{16,0},{1,17},{17,1},{2,18},{18,2},{3,19},{19,3},{4,20},{20... | collective-permute-start | bytes 49160 | tf_op jit(solution)/shard_map/ppermute | solution.py:158

commit v4 on v2

v4 whole, which is shorter than its diff:
```python
import jax
import jax.numpy as jnp
from jax import lax
from jax.experimental import pallas as pl
from jax.experimental.pallas import tpu as pltpu
from jax.sharding import PartitionSpec as P

LANES = 128
PARTS = 2
SMALL = 2.0**-22
RAISE_SMALL = 2.0**37
RAISE = 2.0**8
CLOSE_BYTES = 1 << 19


def fits(array):
    return array.size * jnp.dtype(array.dtype).itemsize <= CLOSE_BYTES


def in_vmem(array):
    return pltpu.with_memory_space_constraint(array, pltpu.VMEM) if fits(array) else array


def result(shape, dtype):
    plain = jax.ShapeDtypeStruct(shape, dtype)
    return pltpu.VMEM(shape, dtype) if fits(plain) else plain


def decode_kernel(part, codes_hbm, centroids_hbm, values_ref, norm_ref, codes_ref, centroids_ref, semaphores):
    spaces, width, centers = centroids_ref.shape
    count = codes_ref.shape[1]
    first = part * spaces
    groups = spaces // 8
    copies = [pltpu.make_async_copy(codes_hbm.at[pl.ds(first, spaces)], codes_ref, semaphores.at[groups])]
    for group in range(groups):
        here = pl.ds(group * 8, 8)
        copies.append(
            pltpu.make_async_copy(
                centroids_hbm.at[pl.ds(first + group * 8, 8)], centroids_ref.at[here], semaphores.at[group]
            )
        )
    for copy in copies:
        copy.start()
    norm_ref[...] = jnp.zeros(norm_ref.shape, jnp.float32)
    copies[0].wait()

    def some_spaces(group, carry):
        here = pl.ds(pl.multiple_of(group * 8, 8), 8)
        pltpu.make_async_copy(centroids_hbm.at[here], centroids_ref.at[here], semaphores.at[group]).wait()
        for tile in range(count // LANES):
            lanes = pl.ds(tile * LANES, LANES)
            code_rows = codes_ref[here, lanes]
            squares = jnp.zeros((8, LANES), jnp.float32)
            for member in range(8):
                space = group * 8 + member
                codes = jnp.broadcast_to(code_rows[member : member + 1], (8, LANES))
                within = codes & (LANES - 1)
                part = codes >> (LANES.bit_length() - 1)
                pieces = []
                for row in range(0, width, 8):
                    value = None
                    for piece in range(centers // LANES):
                        table = centroids_ref[space, pl.ds(row, 8), pl.ds(piece * LANES, LANES)]
                        found = jnp.take_along_axis(table, within, axis=1)
                        value = found if piece == 0 else jnp.where(part == piece, found, value)
                    squares = squares + value * value
                    pieces.append(value)
                values = jnp.concatenate(pieces, axis=0)
                high = values.astype(jnp.bfloat16)
                start = pl.multiple_of(space * width, width)
                values_ref[pl.ds(start, width), lanes] = high
                rest = (values - high.astype(jnp.float32)).astype(jnp.bfloat16)
                values_ref[pl.ds(start + spaces * width, width), lanes] = rest
            norm_ref[:, lanes] += squares
        return carry

    lax.fori_loop(0, groups, some_spaces, 0)


def decode(part, code_ids, centroids):
    spaces, width, centers = centroids.shape
    spaces = spaces // PARTS
    count = code_ids.shape[1]
    return pl.pallas_call(
        lambda *refs: decode_kernel(part, *refs),
        in_specs=[pl.BlockSpec(memory_space=pl.ANY)] * 2,
        out_shape=(
            result((2 * spaces * width, count), jnp.bfloat16),
            result((8, count), jnp.float32),
        ),
        scratch_shapes=[
            pltpu.VMEM((spaces, count), jnp.int32),
            pltpu.VMEM((spaces, width, centers), jnp.float32),
            pltpu.SemaphoreType.DMA((spaces // 8 + 1,)),
        ],
        name="decode",
    )(code_ids, centroids)


def pick_kernel(own_rows, masks, order_ref, mine_ref, theirs_ref):
    half = lax.axis_index("sub")
    own = lax.axis_index("blk")
    place = lax.broadcasted_iota(jnp.int32, mine_ref.shape[::-1], 0)
    slot = place // own_rows
    holder = jnp.full(place.shape, own, jnp.int32)
    for bit, mask in enumerate(masks):
        holder = holder ^ (((slot >> bit) & 1) * mask)
    name = holder * own_rows + place % own_rows
    for pick_ref, side in ((mine_ref, half), (theirs_ref, 1 - half)):
        pick = jnp.where(name == order_ref[pl.ds(side, 1), :], -2.0, 0.0)
        pick_ref[...] = pick.T.astype(jnp.bfloat16)


def make_picks(own_rows, masks, order):
    shape = result((order.shape[1], order.size), jnp.bfloat16)
    return pl.pallas_call(
        lambda *refs: pick_kernel(own_rows, masks, *refs),
        out_shape=(shape, shape),
        name="picks",
    )(order)


def distance_kernel(send, pick_ref, queries_ref, *refs):
    left = jnp.dot(pick_ref[...], queries_ref[...], preferred_element_type=jnp.float32)
    total = 0.25 * jnp.sum(left * left, axis=1, keepdims=True)
    left = left.astype(jnp.bfloat16)
    for part in range(PARTS):
        total = total + jnp.sum(refs[2 * part + 1][...], axis=0, keepdims=True)
    for part in range(PARTS):
        columns = refs[2 * part].shape[0] // 2
        piece = left[:, part * columns : (part + 1) * columns]
        twice = jnp.concatenate([piece, piece], axis=1)
        total = total + jnp.dot(twice, refs[2 * part][...], preferred_element_type=jnp.float32)
    total = jnp.maximum(total, 0.0)
    if send:
        total = jnp.where(total < SMALL, total * -RAISE_SMALL, total * RAISE)
    refs[-1][...] = total


def distances_of(pick, queries, vectors, send):
    return pl.pallas_call(
        lambda *refs: distance_kernel(send, *refs), out_shape=result((pick.shape[0], vectors[0].shape[1]), jnp.float32)
    )(*[in_vmem(array) for array in (pick, queries, *vectors)])


def solution(mesh):
    blocks = mesh.shape["blk"]
    halves = mesh.shape["sub"]
    masks = []
    while (1 << len(masks)) < blocks:
        masks.append((blocks >> (len(masks) + 1)) | 1)

    def local(queries, centroids, code_ids, query_order):
        own_rows = queries.shape[0]
        rows = queries.astype(jnp.bfloat16)
        for mask in masks:
            arrived = lax.ppermute(rows, "blk", [(i, i ^ mask) for i in range(blocks)])
            rows = jnp.concatenate([rows, arrived], axis=0)
        pick_mine, pick_theirs = make_picks(own_rows, masks, query_order.reshape(halves, -1))
        vectors = []
        for part in range(PARTS):
            vectors.extend(decode(part, code_ids, centroids))
        theirs = distances_of(pick_theirs, rows, vectors, True)
        arrived = lax.ppermute(theirs.astype(jnp.float16), "sub", [(i, i ^ 1) for i in range(halves)])
        mine = distances_of(pick_mine, rows, vectors, False)
        arrived = arrived.astype(jnp.float32)
        return mine + arrived * jnp.where(arrived < 0.0, -1.0 / RAISE_SMALL, 1.0 / RAISE)

    in_specs = (P("blk", "sub"), P("sub", None, None), P("sub", "blk"), P())
    return jax.shard_map(local, mesh=mesh, in_specs=in_specs, out_specs=P("sub", "blk"), check_vma=False)
```

time: 27 us -> 24.3 us (0.900)
  waiting for transfers between devices: 11.3 us -> 8.55 us
    ppermute x1, waiting for transfers between devices: 6.6 us -> 3.81 us  [local(): lax.ppermute(theirs.astype(jnp.float16), 'sub', [(i, i ^ 1) for i in rang...]
  transfers between devices with their start and end apart: 5 -> 5, of which waited for: 4 -> 4; matrix products, arithmetic and copies ran while one was open for 0% -> 0% of each run, Pallas kernels for 16% -> 18%
where the time goes in v4:
time: 24.3 us; the launch traced here: 24.1 us
  starting transfers between devices  9 us (37%)
  waiting for transfers between devices  8.55 us (35%)
  Pallas kernels  4.89 us (20%)
  other arithmetic  1.55 us (6%)
    ppermute x4, starting transfers between devices, local(): arrived = lax.ppermute(rows, 'blk', [(i, i ^ mask) for i in range(blocks)])  7.41 us
    ppermute x4, waiting for transfers between devices, local(): arrived = lax.ppermute(rows, 'blk', [(i, i ^ mask) for i in range(blocks)])  4.74 us
    ppermute x1, waiting for transfers between devices, local(): lax.ppermute(theirs.astype(jnp.float16), 'sub', [(i, i ^ 1) for i in rang...  3.81 us
    pallas_call x2, Pallas kernels, decode(): pl.pallas_call(lambda *refs: decode_kernel(part, *refs), in_specs=[pl.Blo...  3.14 us
    ppermute x1, starting transfers between devices, local(): lax.ppermute(theirs.astype(jnp.float16), 'sub', [(i, i ^ 1) for i in rang...  1.59 us
    pallas_call x2, Pallas kernels, distances_of(): pl.pallas_call(lambda *refs: distance_kernel(send, *refs), out_shape=resu...  0.89 us
    pallas_call x1, Pallas kernels, make_picks(): pl.pallas_call(lambda *refs: pick_kernel(own_rows, masks, *refs), out_sha...  0.86 us
    unnamed x1, other arithmetic  0.76 us
  transfers between devices with their start and end apart: 5, of which 4 were waited for; matrix products, arithmetic and copies ran while one was open for 0% of the time, Pallas kernels for 18%

profile of v4, /device:TPU:0, one launch (start us, length us, event | category | flops | bytes accessed | tf_op | source)
XLA Modules:
  0.0 24.1 jit_solution(13872729594539901056)
XLA Ops:
  0.0 0.8 %constant_dynamic-update-slice_fusion.4 = (bf16[256,512]{1,0:T(8,128)(2,1)S(1)}, bf16[16,512]{1,0:T(8,128)(2,1)S(1)}) fusion(f32[16,512]{1,0:T(8,128)} %param.4), kind=kLoop, calls=%fused_computation.10 | loop fusion | flops 8191 | bytes 65536
  0.8 3.5 %collective-permute-start = (bf16[16,512]{1,0:T(8,128)(2,1)S(1)}, bf16[16,512]{1,0:T(8,128)(2,1)S(1)}, u32[]{:S(2)}, u32[]{:S(2)}) collective-permute-start(bf16[16,512]{1,0:T(8,128)(2,1)S(1)} %get-tuple-element.18), channel_id=1, source_target_pairs={{0,9},{1,8},{2,11},{3,10},{4,13},{5,12},{6,15},{7,14},{8,1},{9,0},... | collective-permute-start | bytes 49160 | tf_op jit(solution)/shard_map/ppermute | solution.py:157
  4.3 1.4 %collective-permute-done = bf16[16,512]{1,0:T(8,128)(2,1)S(1)} collective-permute-done((bf16[16,512]{1,0:T(8,128)(2,1)S(1)}, bf16[16,512]{1,0:T(8,128)(2,1)S(1)}, u32[]{:S(2)}, u32[]{:S(2)}) %collective-permute-start) | collective-permute-done | bytes 16416 | tf_op jit(solution)/shard_map/ppermute | solution.py:157
  5.7 1.9 %collective-permute-start.1 = (bf16[32,512]{1,0:T(8,128)(2,1)S(1)}, bf16[32,512]{1,0:T(8,128)(2,1)S(1)}, u32[]{:S(2)}, u32[]{:S(2)}) collective-permute-start(bf16[32,512]{1,0:T(8,128)(2,1)S(1)} %pad_maximum_fusion.2), channel_id=1, source_target_pairs={{0,5},{1,4},{2,7},{3,6},{4,1},{5,0},{6,3},{7,2},{8,13},{9,12},{10,... | collective-permute-start | bytes 98312 | tf_op jit(solution)/shard_map/ppermute | solution.py:157
  7.6 1.6 %decode.2 = (bf16[512,512]{1,0:T(8,128)(2,1)S(1)}, f32[8,512]{1,0:T(8,128)S(1)}) custom-call(s32[32,512]{1,0:T(8,128)} %refs_0_.3, f32[32,16,256]{2,1,0:T(8,128)} %refs_1_.3), custom_call_target="tpu_custom_call" | custom-call | tf_op jit(solution)/shard_map/decode/pallas_call | solution.py:84
  9.2 1.6 %decode.3 = (bf16[512,512]{1,0:T(8,128)(2,1)S(1)}, f32[8,512]{1,0:T(8,128)S(1)}) custom-call(s32[32,512]{1,0:T(8,128)} %refs_0_.3, f32[32,16,256]{2,1,0:T(8,128)} %refs_1_.3), custom_call_target="tpu_custom_call" | custom-call | tf_op jit(solution)/shard_map/decode/pallas_call | solution.py:84
  10.8 0.9 %picks.1 = (bf16[128,256]{1,0:T(8,128)(2,1)S(1)}, bf16[128,256]{1,0:T(8,128)(2,1)S(1)}) custom-call(s32[2,128]{1,0:T(2,128)} %bitcast.1), custom_call_target="tpu_custom_call" | custom-call | tf_op jit(solution)/shard_map/picks/pallas_call | solution.py:116
  11.6 0.0 collective-permute-done.1
  11.6 1.6 %collective-permute-start.2 = (bf16[64,512]{1,0:T(8,128)(2,1)S(1)}, bf16[64,512]{1,0:T(8,128)(2,1)S(1)}, u32[]{:S(2)}, u32[]{:S(2)}) collective-permute-start(bf16[64,512]{1,0:T(8,128)(2,1)S(1)} %pad_maximum_fusion.1), channel_id=1, source_target_pairs={{0,3},{1,2},{2,1},{3,0},{4,7},{5,6},{6,5},{7,4},{8,11},{9,10},{10,... | collective-permute-start | bytes 196616 | tf_op jit(solution)/shard_map/ppermute | solution.py:157
  13.2 2.3 %collective-permute-done.2 = bf16[64,512]{1,0:T(8,128)(2,1)S(1)} collective-permute-done((bf16[64,512]{1,0:T(8,128)(2,1)S(1)}, bf16[64,512]{1,0:T(8,128)(2,1)S(1)}, u32[]{:S(2)}, u32[]{:S(2)}) %collective-permute-start.2) | collective-permute-done | bytes 65568 | tf_op jit(solution)/shard_map/ppermute | solution.py:157
  15.5 0.5 %collective-permute-start.3 = (bf16[128,512]{1,0:T(8,128)(2,1)S(1)}, bf16[128,512]{1,0:T(8,128)(2,1)S(1)}, u32[]{:S(2)}, u32[]{:S(2)}) collective-permute-start(bf16[128,512]{1,0:T(8,128)(2,1)S(1)} %pad_maximum_fusion), channel_id=1, source_target_pairs={{0,1},{1,0},{2,3},{3,2},{4,5},{5,4},{6,7},{7,6},{8,9},{9,8},{10,11... | collective-permute-start | bytes 393224 | tf_op jit(solution)/shard_map/ppermute | solution.py:157
  16.0 1.0 %collective-permute-done.3 = bf16[128,512]{1,0:T(8,128)(2,1)S(1)} collective-permute-done((bf16[128,512]{1,0:T(8,128)(2,1)S(1)}, bf16[128,512]{1,0:T(8,128)(2,1)S(1)}, u32[]{:S(2)}, u32[]{:S(2)}) %collective-permute-start.3) | collective-permute-done | bytes 131104 | tf_op jit(solution)/shard_map/ppermute | solution.py:157
  17.0 0.5 %shard_map.47 = f32[128,512]{1,0:T(8,128)S(1)} custom-call(bf16[128,256]{1,0:T(8,128)(2,1)S(1)} %get-tuple-element.16.refs_0_, bf16[256,512]{1,0:T(8,128)(2,1)S(1)} %constant_dynamic-update-slice_fusion.refs_1_, bf16[512,512]{1,0:T(8,128)(2,1)S(1)} %get-tuple-element.12.refs_2_, f32[8,512]{1,0:T(8,128)S(1)} %get-tuple-element.13.refs_3_, ...), custom_call_target="tpu_custom_call" | custom-call | tf_op jit(solution)/shard_map/pallas_call | solution.py:141
  17.5 1.6 %collective-permute-start.4 = (f16[128,512]{1,0:T(8,128)(2,1)S(1)}, f16[128,512]{1,0:T(8,128)(2,1)S(1)}, u32[]{:S(2)}, u32[]{:S(2)}) collective-permute-start(f16[128,512]{1,0:T(8,128)(2,1)S(1)} %convert_element_type.10), channel_id=1, source_target_pairs={{0,16},{16,0},{1,17},{17,1},{2,18},{18,2},{3,19},{19,3},{4,20},{20... | collective-permute-start | bytes 393224 | tf_op jit(solution)/shard_map/ppermute | solution.py:164
  19.1 0.4 %shard_map.46 = f32[128,512]{1,0:T(8,128)S(1)} custom-call(bf16[128,256]{1,0:T(8,128)(2,1)S(1)} %get-tuple-element.11.refs_0_, bf16[256,512]{1,0:T(8,128)(2,1)S(1)} %constant_dynamic-update-slice_fusion.refs_1_, bf16[512,512]{1,0:T(8,128)(2,1)S(1)} %get-tuple-element.12.refs_2_, f32[8,512]{1,0:T(8,128)S(1)} %get-tuple-element.13.refs_3_, ...), custom_call_target="tpu_custom_call" | custom-call | tf_op jit(solution)/shard_map/pallas_call | solution.py:141
  19.5 3.8 %collective-permute-done.4 = f16[128,512]{1,0:T(8,128)(2,1)S(1)} collective-permute-done((f16[128,512]{1,0:T(8,128)(2,1)S(1)}, f16[128,512]{1,0:T(8,128)(2,1)S(1)}, u32[]{:S(2)}, u32[]{:S(2)}) %collective-permute-start.4) | collective-permute-done | bytes 131104 | tf_op jit(solution)/shard_map/ppermute | solution.py:164
  23.3 0.7 %fusion = f32[128,512]{1,0:T(8,128)} fusion(f32[128,512]{1,0:T(8,128)S(1)} %shard_map.46, f16[128,512]{1,0:T(8,128)(2,1)S(1)} %collective-permute-done.4), kind=kLoop, calls=%fused_computation.2 | loop fusion | flops 327680 | bytes 655360 | tf_op jit(solution)/shard_map/add | solution.py:167
  (8 shorter events, 0.1 us)
Async XLA Ops:
  0.8 4.9 %collective-permute-start = (bf16[16,512]{1,0:T(8,128)(2,1)S(1)}, bf16[16,512]{1,0:T(8,128)(2,1)S(1)}, u32[]{:S(2)}, u32[]{:S(2)}) collective-permute-start(bf16[16,512]{1,0:T(8,128)(2,1)S(1)} %get-tuple-element.18), channel_id=1, source_target_pairs={{0,9},{1,8},{2,11},{3,10},{4,13},{5,12},{6,15},{7,14},{8,1},{9,0},... | collective-permute-start | bytes 49160 | tf_op jit(solution)/shard_map/ppermute | solution.py:157
  5.7 5.9 %collective-permute-start.1 = (bf16[32,512]{1,0:T(8,128)(2,1)S(1)}, bf16[32,512]{1,0:T(8,128)(2,1)S(1)}, u32[]{:S(2)}, u32[]{:S(2)}) collective-permute-start(bf16[32,512]{1,0:T(8,128)(2,1)S(1)} %pad_maximum_fusion.2), channel_id=1, source_target_pairs={{0,5},{1,4},{2,7},{3,6},{4,1},{5,0},{6,3},{7,2},{8,13},{9,12},{10,... | collective-permute-start | bytes 98312 | tf_op jit(solution)/shard_map/ppermute | solution.py:157
  11.6 3.9 %collective-permute-start.2 = (bf16[64,512]{1,0:T(8,128)(2,1)S(1)}, bf16[64,512]{1,0:T(8,128)(2,1)S(1)}, u32[]{:S(2)}, u32[]{:S(2)}) collective-permute-start(bf16[64,512]{1,0:T(8,128)(2,1)S(1)} %pad_maximum_fusion.1), channel_id=1, source_target_pairs={{0,3},{1,2},{2,1},{3,0},{4,7},{5,6},{6,5},{7,4},{8,11},{9,10},{10,... | collective-permute-start | bytes 196616 | tf_op jit(solution)/shard_map/ppermute | solution.py:157
  15.5 1.4 %collective-permute-start.3 = (bf16[128,512]{1,0:T(8,128)(2,1)S(1)}, bf16[128,512]{1,0:T(8,128)(2,1)S(1)}, u32[]{:S(2)}, u32[]{:S(2)}) collective-permute-start(bf16[128,512]{1,0:T(8,128)(2,1)S(1)} %pad_maximum_fusion), channel_id=1, source_target_pairs={{0,1},{1,0},{2,3},{3,2},{4,5},{5,4},{6,7},{7,6},{8,9},{9,8},{10,11... | collective-permute-start | bytes 393224 | tf_op jit(solution)/shard_map/ppermute | solution.py:157
  17.5 5.8 %collective-permute-start.4 = (f16[128,512]{1,0:T(8,128)(2,1)S(1)}, f16[128,512]{1,0:T(8,128)(2,1)S(1)}, u32[]{:S(2)}, u32[]{:S(2)}) collective-permute-start(f16[128,512]{1,0:T(8,128)(2,1)S(1)} %convert_element_type.10), channel_id=1, source_target_pairs={{0,16},{16,0},{1,17},{17,1},{2,18},{18,2},{3,19},{19,3},{4,20},{20... | collective-permute-start | bytes 393224 | tf_op jit(solution)/shard_map/ppermute | solution.py:164

commit v5 on v4

--- a/solution.py
+++ b/solution.py
@@ -26,30 +26,25 @@
     return pltpu.VMEM(shape, dtype) if fits(plain) else plain
 
 
-def decode_kernel(part, codes_hbm, centroids_hbm, values_ref, norm_ref, codes_ref, centroids_ref, semaphores):
+def decode_kernel(part, codes_ref, centroids_hbm, values_ref, norm_ref, centroids_ref, semaphores):
     spaces, width, centers = centroids_ref.shape
     count = codes_ref.shape[1]
     first = part * spaces
     groups = spaces // 8
-    copies = [pltpu.make_async_copy(codes_hbm.at[pl.ds(first, spaces)], codes_ref, semaphores.at[groups])]
     for group in range(groups):
-        here = pl.ds(group * 8, 8)
-        copies.append(
-            pltpu.make_async_copy(
-                centroids_hbm.at[pl.ds(first + group * 8, 8)], centroids_ref.at[here], semaphores.at[group]
-            )
-        )
-    for copy in copies:
-        copy.start()
+        pltpu.make_async_copy(
+            centroids_hbm.at[pl.ds(first + group * 8, 8)],
+            centroids_ref.at[pl.ds(group * 8, 8)],
+            semaphores.at[group],
+        ).start()
     norm_ref[...] = jnp.zeros(norm_ref.shape, jnp.float32)
-    copies[0].wait()
 
     def some_spaces(group, carry):
         here = pl.ds(pl.multiple_of(group * 8, 8), 8)
         pltpu.make_async_copy(centroids_hbm.at[here], centroids_ref.at[here], semaphores.at[group]).wait()
         for tile in range(count // LANES):
             lanes = pl.ds(tile * LANES, LANES)
-            code_rows = codes_ref[here, lanes]
+            code_rows = codes_ref[pl.ds(pl.multiple_of(first + group * 8, 8), 8), lanes]
             squares = jnp.zeros((8, LANES), jnp.float32)
             for member in range(8):
                 space = group * 8 + member
@@ -83,18 +78,17 @@
     count = code_ids.shape[1]
     return pl.pallas_call(
         lambda *refs: decode_kernel(part, *refs),
-        in_specs=[pl.BlockSpec(memory_space=pl.ANY)] * 2,
+        in_specs=[pl.BlockSpec(memory_space=pltpu.VMEM), pl.BlockSpec(memory_space=pl.ANY)],
         out_shape=(
             result((2 * spaces * width, count), jnp.bfloat16),
             result((8, count), jnp.float32),
         ),
         scratch_shapes=[
-            pltpu.VMEM((spaces, count), jnp.int32),
             pltpu.VMEM((spaces, width, centers), jnp.float32),
-            pltpu.SemaphoreType.DMA((spaces // 8 + 1,)),
+            pltpu.SemaphoreType.DMA((spaces // 8,)),
         ],
         name="decode",
-    )(code_ids, centroids)
+    )(in_vmem(code_ids), centroids)
 
 
 def pick_kernel(own_rows, masks, order_ref, mine_ref, theirs_ref):
@@ -139,7 +133,8 @@
 
 def distances_of(pick, queries, vectors, send):
     return pl.pallas_call(
-        lambda *refs: distance_kernel(send, *refs), out_shape=result((pick.shape[0], vectors[0].shape[1]), jnp.float32)
+        lambda *refs: distance_kernel(send, *refs),
+        out_shape=result((pick.shape[0], vectors[0].shape[1]), jnp.float32),
     )(*[in_vmem(array) for array in (pick, queries, *vectors)])
 
 
@@ -152,6 +147,8 @@
 
     def local(queries, centroids, code_ids, query_order):
         own_rows = queries.shape[0]
+        mate = [(i, i ^ 1) for i in range(blocks)]
+        code_ids = lax.ppermute(code_ids, "blk", mate)
         rows = queries.astype(jnp.bfloat16)
         for mask in masks:
             arrived = lax.ppermute(rows, "blk", [(i, i ^ mask) for i in range(blocks)])
@@ -161,8 +158,10 @@
         for part in range(PARTS):
             vectors.extend(decode(part, code_ids, centroids))
         theirs = distances_of(pick_theirs, rows, vectors, True)
-        arrived = lax.ppermute(theirs.astype(jnp.float16), "sub", [(i, i ^ 1) for i in range(halves)])
+        across = [(i, (i ^ 1) ^ blocks) for i in range(halves * blocks)]
+        arrived = lax.ppermute(theirs.astype(jnp.float16), ("sub", "blk"), across)
         mine = distances_of(pick_mine, rows, vectors, False)
+        mine = lax.ppermute(mine, "blk", mate)
         arrived = arrived.astype(jnp.float32)
         return mine + arrived * jnp.where(arrived < 0.0, -1.0 / RAISE_SMALL, 1.0 / RAISE)
 

time: 24.3 us -> 24.4 us (level)
  starting transfers between devices: 9 us -> 10.1 us
  waiting for transfers between devices: 8.55 us -> 7.56 us
    ppermute x1 -> x3, starting transfers between devices: 1.59 us -> 2.67 us  [the longest x1 2.01 us: local(): arrived = lax.ppermute(theirs.astype(jnp.float16), ('sub', 'blk'), across)]
    ppermute x4, waiting for transfers between devices: 4.74 us -> 3.98 us  [local(): arrived = lax.ppermute(rows, 'blk', [(i, i ^ mask) for i in range(blocks)])]
    ppermute x1 -> x3, waiting for transfers between devices: 3.81 us -> 3.58 us  [the longest x1 3.58 us: local(): arrived = lax.ppermute(theirs.astype(jnp.float16), ('sub', 'blk'), across)]
  transfers between devices with their start and end apart: 5 -> 7, of which waited for: 4 -> 4; matrix products, arithmetic and copies ran while one was open for 0% -> 0% of each run, Pallas kernels for 18% -> 18%
where the time goes in v5:
time: 24.4 us; the launch traced here: 24.2 us
  starting transfers between devices  10.1 us (41%)
  waiting for transfers between devices  7.56 us (31%)
  Pallas kernels  4.83 us (20%)
  other arithmetic  1.58 us (6%)
    ppermute x4, starting transfers between devices, local(): arrived = lax.ppermute(rows, 'blk', [(i, i ^ mask) for i in range(blocks)])  7.48 us
    ppermute x4, waiting for transfers between devices, local(): arrived = lax.ppermute(rows, 'blk', [(i, i ^ mask) for i in range(blocks)])  3.98 us
    ppermute x1, waiting for transfers between devices, local(): arrived = lax.ppermute(theirs.astype(jnp.float16), ('sub', 'blk'), across)  3.58 us
    pallas_call x2, Pallas kernels, decode(): pl.pallas_call(lambda *refs: decode_kernel(part, *refs), in_specs=[pl.Blo...  3.08 us
    ppermute x1, starting transfers between devices, local(): arrived = lax.ppermute(theirs.astype(jnp.float16), ('sub', 'blk'), across)  2.01 us
    pallas_call x2, Pallas kernels, distances_of(): pl.pallas_call(lambda *refs: distance_kernel(send, *refs), out_shape=resu...  0.88 us
    pallas_call x1, Pallas kernels, make_picks(): pl.pallas_call(lambda *refs: pick_kernel(own_rows, masks, *refs), out_sha...  0.86 us
    unnamed x1, other arithmetic  0.79 us
  transfers between devices with their start and end apart: 7, of which 4 were waited for; matrix products, arithmetic and copies ran while one was open for 0% of the time, Pallas kernels for 18%

profile of v5, /device:TPU:0, one launch (start us, length us, event | category | flops | bytes accessed | tf_op | source)
XLA Modules:
  0.0 24.2 jit_solution(10159832948225987577)
XLA Ops:
  0.0 0.0 copy-start
  0.0 0.8 %constant_dynamic-update-slice_fusion.4 = (bf16[256,512]{1,0:T(8,128)(2,1)S(1)}, bf16[16,512]{1,0:T(8,128)(2,1)S(1)}) fusion(f32[16,512]{1,0:T(8,128)} %param.4), kind=kLoop, calls=%fused_computation.10 | loop fusion | flops 8191 | bytes 65536
  0.8 3.5 %collective-permute-start = (bf16[16,512]{1,0:T(8,128)(2,1)S(1)}, bf16[16,512]{1,0:T(8,128)(2,1)S(1)}, u32[]{:S(2)}, u32[]{:S(2)}) collective-permute-start(bf16[16,512]{1,0:T(8,128)(2,1)S(1)} %get-tuple-element.18), channel_id=1, source_target_pairs={{0,9},{1,8},{2,11},{3,10},{4,13},{5,12},{6,15},{7,14},{8,1},{9,0},... | collective-permute-start | bytes 49160 | tf_op jit(solution)/shard_map/ppermute | solution.py:154
  4.3 1.4 %collective-permute-done = bf16[16,512]{1,0:T(8,128)(2,1)S(1)} collective-permute-done((bf16[16,512]{1,0:T(8,128)(2,1)S(1)}, bf16[16,512]{1,0:T(8,128)(2,1)S(1)}, u32[]{:S(2)}, u32[]{:S(2)}) %collective-permute-start) | collective-permute-done | bytes 16416 | tf_op jit(solution)/shard_map/ppermute | solution.py:154
  5.7 1.9 %collective-permute-start.1 = (bf16[32,512]{1,0:T(8,128)(2,1)S(1)}, bf16[32,512]{1,0:T(8,128)(2,1)S(1)}, u32[]{:S(2)}, u32[]{:S(2)}) collective-permute-start(bf16[32,512]{1,0:T(8,128)(2,1)S(1)} %pad_maximum_fusion.2), channel_id=1, source_target_pairs={{0,5},{1,4},{2,7},{3,6},{4,1},{5,0},{6,3},{7,2},{8,13},{9,12},{10,... | collective-permute-start | bytes 98312 | tf_op jit(solution)/shard_map/ppermute | solution.py:154
  7.6 0.0 copy-done
  7.6 0.4 %collective-permute-start.4 = (s32[32,512]{1,0:T(8,128)S(1)}, s32[32,512]{1,0:T(8,128)S(1)}, u32[]{:S(2)}, u32[]{:S(2)}) collective-permute-start(s32[32,512]{1,0:T(8,128)S(1)} %copy-done), channel_id=1, source_target_pairs={{0,1},{1,0},{2,3},{3,2},{4,5},{5,4},{6,7},{7,6},{8,9},{9,8},{10,11... | collective-permute-start | bytes 196616 | tf_op jit(solution)/shard_map/ppermute | solution.py:151
  8.0 0.9 %picks.1 = (bf16[128,256]{1,0:T(8,128)(2,1)S(1)}, bf16[128,256]{1,0:T(8,128)(2,1)S(1)}) custom-call(s32[2,128]{1,0:T(2,128)} %bitcast.1), custom_call_target="tpu_custom_call" | custom-call | tf_op jit(solution)/shard_map/picks/pallas_call | solution.py:110
  8.9 0.3 %collective-permute-done.1 = bf16[32,512]{1,0:T(8,128)(2,1)S(1)} collective-permute-done((bf16[32,512]{1,0:T(8,128)(2,1)S(1)}, bf16[32,512]{1,0:T(8,128)(2,1)S(1)}, u32[]{:S(2)}, u32[]{:S(2)}) %collective-permute-start.1) | collective-permute-done | bytes 32800 | tf_op jit(solution)/shard_map/ppermute | solution.py:154
  9.2 1.7 %collective-permute-start.2 = (bf16[64,512]{1,0:T(8,128)(2,1)S(1)}, bf16[64,512]{1,0:T(8,128)(2,1)S(1)}, u32[]{:S(2)}, u32[]{:S(2)}) collective-permute-start(bf16[64,512]{1,0:T(8,128)(2,1)S(1)} %pad_maximum_fusion.1), channel_id=1, source_target_pairs={{0,3},{1,2},{2,1},{3,0},{4,7},{5,6},{6,5},{7,4},{8,11},{9,10},{10,... | collective-permute-start | bytes 196616 | tf_op jit(solution)/shard_map/ppermute | solution.py:154
  11.0 2.2 %collective-permute-done.2 = bf16[64,512]{1,0:T(8,128)(2,1)S(1)} collective-permute-done((bf16[64,512]{1,0:T(8,128)(2,1)S(1)}, bf16[64,512]{1,0:T(8,128)(2,1)S(1)}, u32[]{:S(2)}, u32[]{:S(2)}) %collective-permute-start.2) | collective-permute-done | bytes 65568 | tf_op jit(solution)/shard_map/ppermute | solution.py:154
  13.2 0.4 %collective-permute-start.3 = (bf16[128,512]{1,0:T(8,128)(2,1)S(1)}, bf16[128,512]{1,0:T(8,128)(2,1)S(1)}, u32[]{:S(2)}, u32[]{:S(2)}) collective-permute-start(bf16[128,512]{1,0:T(8,128)(2,1)S(1)} %pad_maximum_fusion), channel_id=1, source_target_pairs={{0,1},{1,0},{2,3},{3,2},{4,5},{5,4},{6,7},{7,6},{8,9},{9,8},{10,11... | collective-permute-start | bytes 393224 | tf_op jit(solution)/shard_map/ppermute | solution.py:154
  13.5 0.0 collective-permute-done.4.refs_0_
  13.5 1.5 %decode.2 = (bf16[512,512]{1,0:T(8,128)(2,1)S(1)}, f32[8,512]{1,0:T(8,128)S(1)}) custom-call(s32[32,512]{1,0:T(8,128)S(1)} %collective-permute-done.4.refs_0_, f32[32,16,256]{2,1,0:T(8,128)} %refs_1_.3), custom_call_target="tpu_custom_call" | custom-call | tf_op jit(solution)/shard_map/decode/pallas_call | solution.py:79
  15.1 1.5 %decode.3 = (bf16[512,512]{1,0:T(8,128)(2,1)S(1)}, f32[8,512]{1,0:T(8,128)S(1)}) custom-call(s32[32,512]{1,0:T(8,128)S(1)} %collective-permute-done.4.refs_0_, f32[32,16,256]{2,1,0:T(8,128)} %refs_1_.3), custom_call_target="tpu_custom_call" | custom-call | tf_op jit(solution)/shard_map/decode/pallas_call | solution.py:79
  16.7 0.0 collective-permute-done.3
  16.7 0.4 %shard_map.46 = f32[128,512]{1,0:T(8,128)S(1)} custom-call(bf16[128,256]{1,0:T(8,128)(2,1)S(1)} %get-tuple-element.11.refs_0_, bf16[256,512]{1,0:T(8,128)(2,1)S(1)} %constant_dynamic-update-slice_fusion.refs_1_, bf16[512,512]{1,0:T(8,128)(2,1)S(1)} %get-tuple-element.12.refs_2_, f32[8,512]{1,0:T(8,128)S(1)} %get-tuple-element.13.refs_3_, ...), custom_call_target="tpu_custom_call" | custom-call | tf_op jit(solution)/shard_map/pallas_call | solution.py:135
  17.1 0.3 %collective-permute-start.5 = (f32[128,512]{1,0:T(8,128)S(1)}, f32[128,512]{1,0:T(8,128)S(1)}, u32[]{:S(2)}, u32[]{:S(2)}) collective-permute-start(f32[128,512]{1,0:T(8,128)S(1)} %shard_map.46), channel_id=1, source_target_pairs={{0,1},{1,0},{2,3},{3,2},{4,5},{5,4},{6,7},{7,6},{8,9},{9,8},{10,11... | collective-permute-start | bytes 786440 | tf_op jit(solution)/shard_map/ppermute | solution.py:164
  17.4 0.5 %shard_map.47 = f32[128,512]{1,0:T(8,128)S(1)} custom-call(bf16[128,256]{1,0:T(8,128)(2,1)S(1)} %get-tuple-element.16.refs_0_, bf16[256,512]{1,0:T(8,128)(2,1)S(1)} %constant_dynamic-update-slice_fusion.refs_1_, bf16[512,512]{1,0:T(8,128)(2,1)S(1)} %get-tuple-element.12.refs_2_, f32[8,512]{1,0:T(8,128)S(1)} %get-tuple-element.13.refs_3_, ...), custom_call_target="tpu_custom_call" | custom-call | tf_op jit(solution)/shard_map/pallas_call | solution.py:135
  17.9 2.0 %collective-permute-start.6 = (f16[128,512]{1,0:T(8,128)(2,1)S(1)}, f16[128,512]{1,0:T(8,128)(2,1)S(1)}, u32[]{:S(2)}, u32[]{:S(2)}) collective-permute-start(f16[128,512]{1,0:T(8,128)(2,1)S(1)} %convert_element_type.10), channel_id=1, source_target_pairs={{0,17},{1,16},{2,19},{3,18},{4,21},{5,20},{6,23},{7,22},{8,25},{9,... | collective-permute-start | bytes 393224 | tf_op jit(solution)/shard_map/ppermute | solution.py:162
  19.9 3.6 %collective-permute-done.6 = f16[128,512]{1,0:T(8,128)(2,1)S(1)} collective-permute-done((f16[128,512]{1,0:T(8,128)(2,1)S(1)}, f16[128,512]{1,0:T(8,128)(2,1)S(1)}, u32[]{:S(2)}, u32[]{:S(2)}) %collective-permute-start.6) | collective-permute-done | bytes 131104 | tf_op jit(solution)/shard_map/ppermute | solution.py:162
  23.5 0.0 collective-permute-done.5
  23.5 0.7 %fusion = f32[128,512]{1,0:T(8,128)} fusion(f32[128,512]{1,0:T(8,128)S(1)} %collective-permute-done.5, f16[128,512]{1,0:T(8,128)(2,1)S(1)} %collective-permute-done.6), kind=kLoop, calls=%fused_computation.2 | loop fusion | flops 327680 | bytes 655360 | tf_op jit(solution)/shard_map/add | solution.py:166
  (8 shorter events, 0.1 us)
Async XLA Ops:
  0.0 7.6 %copy-start = (s32[32,512]{1,0:T(8,128)S(1)}, s32[32,512]{1,0:T(8,128)}, u32[]{:S(2)}) copy-start(s32[32,512]{1,0:T(8,128)} %param.6) | copy-start | bytes 196612
  0.8 4.9 %collective-permute-start = (bf16[16,512]{1,0:T(8,128)(2,1)S(1)}, bf16[16,512]{1,0:T(8,128)(2,1)S(1)}, u32[]{:S(2)}, u32[]{:S(2)}) collective-permute-start(bf16[16,512]{1,0:T(8,128)(2,1)S(1)} %get-tuple-element.18), channel_id=1, source_target_pairs={{0,9},{1,8},{2,11},{3,10},{4,13},{5,12},{6,15},{7,14},{8,1},{9,0},... | collective-permute-start | bytes 49160 | tf_op jit(solution)/shard_map/ppermute | solution.py:154
  5.7 3.5 %collective-permute-start.1 = (bf16[32,512]{1,0:T(8,128)(2,1)S(1)}, bf16[32,512]{1,0:T(8,128)(2,1)S(1)}, u32[]{:S(2)}, u32[]{:S(2)}) collective-permute-start(bf16[32,512]{1,0:T(8,128)(2,1)S(1)} %pad_maximum_fusion.2), channel_id=1, source_target_pairs={{0,5},{1,4},{2,7},{3,6},{4,1},{5,0},{6,3},{7,2},{8,13},{9,12},{10,... | collective-permute-start | bytes 98312 | tf_op jit(solution)/shard_map/ppermute | solution.py:154
  7.6 5.9 %collective-permute-start.4 = (s32[32,512]{1,0:T(8,128)S(1)}, s32[32,512]{1,0:T(8,128)S(1)}, u32[]{:S(2)}, u32[]{:S(2)}) collective-permute-start(s32[32,512]{1,0:T(8,128)S(1)} %copy-done), channel_id=1, source_target_pairs={{0,1},{1,0},{2,3},{3,2},{4,5},{5,4},{6,7},{7,6},{8,9},{9,8},{10,11... | collective-permute-start | bytes 196616 | tf_op jit(solution)/shard_map/ppermute | solution.py:151
  9.2 3.9 %collective-permute-start.2 = (bf16[64,512]{1,0:T(8,128)(2,1)S(1)}, bf16[64,512]{1,0:T(8,128)(2,1)S(1)}, u32[]{:S(2)}, u32[]{:S(2)}) collective-permute-start(bf16[64,512]{1,0:T(8,128)(2,1)S(1)} %pad_maximum_fusion.1), channel_id=1, source_target_pairs={{0,3},{1,2},{2,1},{3,0},{4,7},{5,6},{6,5},{7,4},{8,11},{9,10},{10,... | collective-permute-start | bytes 196616 | tf_op jit(solution)/shard_map/ppermute | solution.py:154
  13.2 3.5 %collective-permute-start.3 = (bf16[128,512]{1,0:T(8,128)(2,1)S(1)}, bf16[128,512]{1,0:T(8,128)(2,1)S(1)}, u32[]{:S(2)}, u32[]{:S(2)}) collective-permute-start(bf16[128,512]{1,0:T(8,128)(2,1)S(1)} %pad_maximum_fusion), channel_id=1, source_target_pairs={{0,1},{1,0},{2,3},{3,2},{4,5},{5,4},{6,7},{7,6},{8,9},{9,8},{10,11... | collective-permute-start | bytes 393224 | tf_op jit(solution)/shard_map/ppermute | solution.py:154
  17.1 6.3 %collective-permute-start.5 = (f32[128,512]{1,0:T(8,128)S(1)}, f32[128,512]{1,0:T(8,128)S(1)}, u32[]{:S(2)}, u32[]{:S(2)}) collective-permute-start(f32[128,512]{1,0:T(8,128)S(1)} %shard_map.46), channel_id=1, source_target_pairs={{0,1},{1,0},{2,3},{3,2},{4,5},{5,4},{6,7},{7,6},{8,9},{9,8},{10,11... | collective-permute-start | bytes 786440 | tf_op jit(solution)/shard_map/ppermute | solution.py:164
  17.9 5.6 %collective-permute-start.6 = (f16[128,512]{1,0:T(8,128)(2,1)S(1)}, f16[128,512]{1,0:T(8,128)(2,1)S(1)}, u32[]{:S(2)}, u32[]{:S(2)}) collective-permute-start(f16[128,512]{1,0:T(8,128)(2,1)S(1)} %convert_element_type.10), channel_id=1, source_target_pairs={{0,17},{1,16},{2,19},{3,18},{4,21},{5,20},{6,23},{7,22},{8,25},{9,... | collective-permute-start | bytes 393224 | tf_op jit(solution)/shard_map/ppermute | solution.py:162

commit v6 on v5

--- a/solution.py
+++ b/solution.py
@@ -10,6 +10,7 @@
 SMALL = 2.0**-22
 RAISE_SMALL = 2.0**37
 RAISE = 2.0**8
+STRETCH = 163840.0
 CLOSE_BYTES = 1 << 19
 
 
@@ -101,7 +102,7 @@
         holder = holder ^ (((slot >> bit) & 1) * mask)
     name = holder * own_rows + place % own_rows
     for pick_ref, side in ((mine_ref, half), (theirs_ref, 1 - half)):
-        pick = jnp.where(name == order_ref[pl.ds(side, 1), :], -2.0, 0.0)
+        pick = jnp.where(name == order_ref[pl.ds(side, 1), :], 1.0, 0.0)
         pick_ref[...] = pick.T.astype(jnp.bfloat16)
 
 
@@ -114,18 +115,32 @@
     )(order)
 
 
-def distance_kernel(send, pick_ref, queries_ref, *refs):
-    left = jnp.dot(pick_ref[...], queries_ref[...], preferred_element_type=jnp.float32)
-    total = 0.25 * jnp.sum(left * left, axis=1, keepdims=True)
-    left = left.astype(jnp.bfloat16)
+def picked(pick_ref, *row_refs):
+    total, first = None, 0
+    for row_ref in row_refs:
+        columns = pick_ref[:, pl.ds(first, row_ref.shape[0])]
+        rows = jnp.dot(columns, row_ref[...], preferred_element_type=jnp.float32)
+        total, first = rows if total is None else total + rows, first + row_ref.shape[0]
+    return total
+
+
+def distance_kernel(send, pick_ref, high_ref, low_ref, mate_high_ref, mate_low_ref, *refs):
+    high = picked(pick_ref, high_ref, mate_high_ref)
+    low = picked(pick_ref, low_ref, mate_low_ref)
+    whole = high + low
+    rows = whole.shape[0]
+    both = jnp.concatenate([high, low], axis=0).astype(jnp.bfloat16)
+    cross = jnp.zeros((rows, refs[-1].shape[1]), jnp.float32)
+    total = (1.0 / STRETCH**2) * jnp.sum(whole * whole, axis=1, keepdims=True)
     for part in range(PARTS):
         total = total + jnp.sum(refs[2 * part + 1][...], axis=0, keepdims=True)
     for part in range(PARTS):
         columns = refs[2 * part].shape[0] // 2
-        piece = left[:, part * columns : (part + 1) * columns]
-        twice = jnp.concatenate([piece, piece], axis=1)
-        total = total + jnp.dot(twice, refs[2 * part][...], preferred_element_type=jnp.float32)
-    total = jnp.maximum(total, 0.0)
+        piece = both[:, part * columns : (part + 1) * columns]
+        product = jnp.dot(piece, refs[2 * part][:columns], preferred_element_type=jnp.float32)
+        cross = cross + (product[:rows] + product[rows:])
+        cross = cross + jnp.dot(piece[:rows], refs[2 * part][columns:], preferred_element_type=jnp.float32)
+    total = jnp.maximum(total - (2.0 / STRETCH) * cross, 0.0)
     if send:
         total = jnp.where(total < SMALL, total * -RAISE_SMALL, total * RAISE)
     refs[-1][...] = total
@@ -135,7 +150,13 @@
     return pl.pallas_call(
         lambda *refs: distance_kernel(send, *refs),
         out_shape=result((pick.shape[0], vectors[0].shape[1]), jnp.float32),
-    )(*[in_vmem(array) for array in (pick, queries, *vectors)])
+    )(*[in_vmem(array) for array in (pick, *queries, *vectors)])
+
+
+def split(rows):
+    rows = rows.astype(jnp.float32)
+    high = lax.reduce_precision(rows, 8, 7)
+    return high.astype(jnp.bfloat16), (rows - high).astype(jnp.bfloat16)
 
 
 def solution(mesh):
@@ -149,18 +170,21 @@
         own_rows = queries.shape[0]
         mate = [(i, i ^ 1) for i in range(blocks)]
         code_ids = lax.ppermute(code_ids, "blk", mate)
-        rows = queries.astype(jnp.bfloat16)
-        for mask in masks:
+        rows = (queries * STRETCH).astype(jnp.float16)
+        for step, mask in enumerate(masks):
             arrived = lax.ppermute(rows, "blk", [(i, i ^ mask) for i in range(blocks)])
-            rows = jnp.concatenate([rows, arrived], axis=0)
+            if step + 1 < len(masks):
+                rows = jnp.concatenate([rows, arrived], axis=0)
+            else:
+                queries = (*split(rows), *split(arrived))
         pick_mine, pick_theirs = make_picks(own_rows, masks, query_order.reshape(halves, -1))
         vectors = []
         for part in range(PARTS):
             vectors.extend(decode(part, code_ids, centroids))
-        theirs = distances_of(pick_theirs, rows, vectors, True)
+        theirs = distances_of(pick_theirs, queries, vectors, True)
         across = [(i, (i ^ 1) ^ blocks) for i in range(halves * blocks)]
         arrived = lax.ppermute(theirs.astype(jnp.float16), ("sub", "blk"), across)
-        mine = distances_of(pick_mine, rows, vectors, False)
+        mine = distances_of(pick_mine, queries, vectors, False)
         mine = lax.ppermute(mine, "blk", mate)
         arrived = arrived.astype(jnp.float32)
         return mine + arrived * jnp.where(arrived < 0.0, -1.0 / RAISE_SMALL, 1.0 / RAISE)

time: 24.4 us -> 25.8 us (1.057)
  waiting for transfers between devices: 7.56 us -> 8.43 us
  Pallas kernels: 4.83 us -> 5.12 us
    ppermute x4, waiting for transfers between devices: 3.98 us -> 4.84 us  [local(): arrived = lax.ppermute(rows, 'blk', [(i, i ^ mask) for i in range(blocks)])]
    convert_element_type x0 -> x3, other arithmetic: none -> 0.86 us  [the longest x1 0.76 us: local(): rows = (queries * STRETCH).astype(jnp.float16)]
    unnamed x1 -> x0, other arithmetic: 0.79 us -> none
    pallas_call x2, Pallas kernels: 0.88 us -> 1.17 us  [distances_of(): pl.pallas_call(lambda *refs: distance_kernel(send, *refs), out_shape=resu...]
where the time goes in v6:
time: 25.8 us; the launch traced here: 25.6 us
  starting transfers between devices  10.3 us (40%)
  waiting for transfers between devices  8.43 us (33%)
  Pallas kernels  5.12 us (20%)
  other arithmetic  1.7 us (7%)
    ppermute x4, starting transfers between devices, local(): arrived = lax.ppermute(rows, 'blk', [(i, i ^ mask) for i in range(blocks)])  7.61 us
    ppermute x4, waiting for transfers between devices, local(): arrived = lax.ppermute(rows, 'blk', [(i, i ^ mask) for i in range(blocks)])  4.84 us
    ppermute x1, waiting for transfers between devices, local(): arrived = lax.ppermute(theirs.astype(jnp.float16), ('sub', 'blk'), across)  3.59 us
    pallas_call x2, Pallas kernels, decode(): pl.pallas_call(lambda *refs: decode_kernel(part, *refs), in_specs=[pl.Blo...  3.09 us
    ppermute x1, starting transfers between devices, local(): arrived = lax.ppermute(theirs.astype(jnp.float16), ('sub', 'blk'), across)  2 us
    pallas_call x2, Pallas kernels, distances_of(): pl.pallas_call(lambda *refs: distance_kernel(send, *refs), out_shape=resu...  1.17 us
    pallas_call x1, Pallas kernels, make_picks(): pl.pallas_call(lambda *refs: pick_kernel(own_rows, masks, *refs), out_sha...  0.86 us
    convert_element_type x1, other arithmetic, local(): rows = (queries * STRETCH).astype(jnp.float16)  0.76 us
  transfers between devices with their start and end apart: 7, of which 4 were waited for; matrix products, arithmetic and copies ran while one was open for 0% of the time, Pallas kernels for 18%

profile of v6, /device:TPU:0, one launch (start us, length us, event | category | flops | bytes accessed | tf_op | source)
XLA Modules:
  0.0 25.6 jit_solution(17818987079638912531)
XLA Ops:
  0.0 0.8 %multiply_convert_fusion = f16[16,512]{1,0:T(8,128)(2,1)S(1)} fusion(f32[16,512]{1,0:T(8,128)} %param.4), kind=kLoop, calls=%fused_computation.12 | loop fusion | flops 16384 | bytes 49152 | tf_op jit(solution)/shard_map/convert_element_type | solution.py:173
  0.8 3.5 %collective-permute-start = (f16[16,512]{1,0:T(8,128)(2,1)S(1)}, f16[16,512]{1,0:T(8,128)(2,1)S(1)}, u32[]{:S(2)}, u32[]{:S(2)}) collective-permute-start(f16[16,512]{1,0:T(8,128)(2,1)S(1)} %multiply_convert_fusion), channel_id=1, source_target_pairs={{0,9},{1,8},{2,11},{3,10},{4,13},{5,12},{6,15},{7,14},{8,1},{9,0},... | collective-permute-start | bytes 49160 | tf_op jit(solution)/shard_map/ppermute | solution.py:175
  4.3 1.4 %collective-permute-done = f16[16,512]{1,0:T(8,128)(2,1)S(1)} collective-permute-done((f16[16,512]{1,0:T(8,128)(2,1)S(1)}, f16[16,512]{1,0:T(8,128)(2,1)S(1)}, u32[]{:S(2)}, u32[]{:S(2)}) %collective-permute-start) | collective-permute-done | bytes 16416 | tf_op jit(solution)/shard_map/ppermute | solution.py:175
  5.7 0.0 copy-start
  5.7 2.0 %collective-permute-start.1 = (f16[32,512]{1,0:T(8,128)(2,1)S(1)}, f16[32,512]{1,0:T(8,128)(2,1)S(1)}, u32[]{:S(2)}, u32[]{:S(2)}) collective-permute-start(f16[32,512]{1,0:T(8,128)(2,1)S(1)} %pad_maximum_fusion.2), channel_id=1, source_target_pairs={{0,5},{1,4},{2,7},{3,6},{4,1},{5,0},{6,3},{7,2},{8,13},{9,12},{10,... | collective-permute-start | bytes 98312 | tf_op jit(solution)/shard_map/ppermute | solution.py:175
  7.7 1.6 %collective-permute-done.1 = f16[32,512]{1,0:T(8,128)(2,1)S(1)} collective-permute-done((f16[32,512]{1,0:T(8,128)(2,1)S(1)}, f16[32,512]{1,0:T(8,128)(2,1)S(1)}, u32[]{:S(2)}, u32[]{:S(2)}) %collective-permute-start.1) | collective-permute-done | bytes 32800 | tf_op jit(solution)/shard_map/ppermute | solution.py:175
  9.3 1.8 %collective-permute-start.2 = (f16[64,512]{1,0:T(8,128)(2,1)S(1)}, f16[64,512]{1,0:T(8,128)(2,1)S(1)}, u32[]{:S(2)}, u32[]{:S(2)}) collective-permute-start(f16[64,512]{1,0:T(8,128)(2,1)S(1)} %pad_maximum_fusion.1), channel_id=1, source_target_pairs={{0,3},{1,2},{2,1},{3,0},{4,7},{5,6},{6,5},{7,4},{8,11},{9,10},{10,... | collective-permute-start | bytes 196616 | tf_op jit(solution)/shard_map/ppermute | solution.py:175
  11.1 0.0 copy-done
  11.1 0.4 %collective-permute-start.4 = (s32[32,512]{1,0:T(8,128)S(1)}, s32[32,512]{1,0:T(8,128)S(1)}, u32[]{:S(2)}, u32[]{:S(2)}) collective-permute-start(s32[32,512]{1,0:T(8,128)S(1)} %copy-done), channel_id=1, source_target_pairs={{0,1},{1,0},{2,3},{3,2},{4,5},{5,4},{6,7},{7,6},{8,9},{9,8},{10,11... | collective-permute-start | bytes 196616 | tf_op jit(solution)/shard_map/ppermute | solution.py:172
  11.5 1.8 %collective-permute-done.2 = f16[64,512]{1,0:T(8,128)(2,1)S(1)} collective-permute-done((f16[64,512]{1,0:T(8,128)(2,1)S(1)}, f16[64,512]{1,0:T(8,128)(2,1)S(1)}, u32[]{:S(2)}, u32[]{:S(2)}) %collective-permute-start.2) | collective-permute-done | bytes 65568 | tf_op jit(solution)/shard_map/ppermute | solution.py:175
  13.3 0.4 %collective-permute-start.3 = (f16[128,512]{1,0:T(8,128)(2,1)S(1)}, f16[128,512]{1,0:T(8,128)(2,1)S(1)}, u32[]{:S(2)}, u32[]{:S(2)}) collective-permute-start(f16[128,512]{1,0:T(8,128)(2,1)S(1)} %pad_maximum_fusion), channel_id=1, source_target_pairs={{0,1},{1,0},{2,3},{3,2},{4,5},{5,4},{6,7},{7,6},{8,9},{9,8},{10,11... | collective-permute-start | bytes 393224 | tf_op jit(solution)/shard_map/ppermute | solution.py:175
  13.7 0.9 %picks.1 = (bf16[128,256]{1,0:T(8,128)(2,1)S(1)}, bf16[128,256]{1,0:T(8,128)(2,1)S(1)}) custom-call(s32[2,128]{1,0:T(2,128)} %bitcast.1), custom_call_target="tpu_custom_call" | custom-call | tf_op jit(solution)/shard_map/picks/pallas_call | solution.py:111
  14.6 0.0 collective-permute-done.4.refs_0_
  14.6 1.5 %decode.2 = (bf16[512,512]{1,0:T(8,128)(2,1)S(1)}, f32[8,512]{1,0:T(8,128)S(1)}) custom-call(s32[32,512]{1,0:T(8,128)S(1)} %collective-permute-done.4.refs_0_, f32[32,16,256]{2,1,0:T(8,128)} %refs_1_.3), custom_call_target="tpu_custom_call" | custom-call | tf_op jit(solution)/shard_map/decode/pallas_call | solution.py:80
  16.1 1.5 %decode.3 = (bf16[512,512]{1,0:T(8,128)(2,1)S(1)}, f32[8,512]{1,0:T(8,128)S(1)}) custom-call(s32[32,512]{1,0:T(8,128)S(1)} %collective-permute-done.4.refs_0_, f32[32,16,256]{2,1,0:T(8,128)} %refs_1_.3), custom_call_target="tpu_custom_call" | custom-call | tf_op jit(solution)/shard_map/decode/pallas_call | solution.py:80
  17.7 0.1 fusion.1
  17.7 0.0 collective-permute-done.3
  17.8 0.6 %shard_map.46 = f32[128,512]{1,0:T(8,128)S(1)} custom-call(bf16[128,256]{1,0:T(8,128)(2,1)S(1)} %get-tuple-element.11.refs_0_, bf16[128,512]{1,0:T(8,128)(2,1)S(1)} %get-tuple-element.20.refs_1_, bf16[128,512]{1,0:T(8,128)(2,1)S(1)} %get-tuple-element.19.refs_2_, bf16[128,512]{1,0:T(8,128)(2,1)S(1)} %get-tuple-element.18.refs_3_, ...), custom_call_target="tpu_custom_call" | custom-call | tf_op jit(solution)/shard_map/pallas_call | solution.py:150
  18.4 0.3 %collective-permute-start.5 = (f32[128,512]{1,0:T(8,128)S(1)}, f32[128,512]{1,0:T(8,128)S(1)}, u32[]{:S(2)}, u32[]{:S(2)}) collective-permute-start(f32[128,512]{1,0:T(8,128)S(1)} %shard_map.46), channel_id=1, source_target_pairs={{0,1},{1,0},{2,3},{3,2},{4,5},{5,4},{6,7},{7,6},{8,9},{9,8},{10,11... | collective-permute-start | bytes 786440 | tf_op jit(solution)/shard_map/ppermute | solution.py:188
  18.6 0.6 %shard_map.47 = f32[128,512]{1,0:T(8,128)S(1)} custom-call(bf16[128,256]{1,0:T(8,128)(2,1)S(1)} %get-tuple-element.16.refs_0_, bf16[128,512]{1,0:T(8,128)(2,1)S(1)} %get-tuple-element.20.refs_1_, bf16[128,512]{1,0:T(8,128)(2,1)S(1)} %get-tuple-element.19.refs_2_, bf16[128,512]{1,0:T(8,128)(2,1)S(1)} %get-tuple-element.18.refs_3_, ...), custom_call_target="tpu_custom_call" | custom-call | tf_op jit(solution)/shard_map/pallas_call | solution.py:150
  19.3 2.0 %collective-permute-start.6 = (f16[128,512]{1,0:T(8,128)(2,1)S(1)}, f16[128,512]{1,0:T(8,128)(2,1)S(1)}, u32[]{:S(2)}, u32[]{:S(2)}) collective-permute-start(f16[128,512]{1,0:T(8,128)(2,1)S(1)} %convert_element_type.34), channel_id=1, source_target_pairs={{0,17},{1,16},{2,19},{3,18},{4,21},{5,20},{6,23},{7,22},{8,25},{9,... | collective-permute-start | bytes 393224 | tf_op jit(solution)/shard_map/ppermute | solution.py:186
  21.3 3.6 %collective-permute-done.6 = f16[128,512]{1,0:T(8,128)(2,1)S(1)} collective-permute-done((f16[128,512]{1,0:T(8,128)(2,1)S(1)}, f16[128,512]{1,0:T(8,128)(2,1)S(1)}, u32[]{:S(2)}, u32[]{:S(2)}) %collective-permute-start.6) | collective-permute-done | bytes 131104 | tf_op jit(solution)/shard_map/ppermute | solution.py:186
  24.9 0.0 collective-permute-done.5
  24.9 0.7 %fusion = f32[128,512]{1,0:T(8,128)} fusion(f32[128,512]{1,0:T(8,128)S(1)} %collective-permute-done.5, f16[128,512]{1,0:T(8,128)(2,1)S(1)} %collective-permute-done.6), kind=kLoop, calls=%fused_computation.6 | loop fusion | flops 327680 | bytes 655360 | tf_op jit(solution)/shard_map/add | solution.py:190
  (5 shorter events, 0.1 us)
Async XLA Ops:
  0.8 4.9 %collective-permute-start = (f16[16,512]{1,0:T(8,128)(2,1)S(1)}, f16[16,512]{1,0:T(8,128)(2,1)S(1)}, u32[]{:S(2)}, u32[]{:S(2)}) collective-permute-start(f16[16,512]{1,0:T(8,128)(2,1)S(1)} %multiply_convert_fusion), channel_id=1, source_target_pairs={{0,9},{1,8},{2,11},{3,10},{4,13},{5,12},{6,15},{7,14},{8,1},{9,0},... | collective-permute-start | bytes 49160 | tf_op jit(solution)/shard_map/ppermute | solution.py:175
  5.7 5.4 %copy-start = (s32[32,512]{1,0:T(8,128)S(1)}, s32[32,512]{1,0:T(8,128)}, u32[]{:S(2)}) copy-start(s32[32,512]{1,0:T(8,128)} %param.6) | copy-start | bytes 196612
  5.7 3.6 %collective-permute-start.1 = (f16[32,512]{1,0:T(8,128)(2,1)S(1)}, f16[32,512]{1,0:T(8,128)(2,1)S(1)}, u32[]{:S(2)}, u32[]{:S(2)}) collective-permute-start(f16[32,512]{1,0:T(8,128)(2,1)S(1)} %pad_maximum_fusion.2), channel_id=1, source_target_pairs={{0,5},{1,4},{2,7},{3,6},{4,1},{5,0},{6,3},{7,2},{8,13},{9,12},{10,... | collective-permute-start | bytes 98312 | tf_op jit(solution)/shard_map/ppermute | solution.py:175
  9.3 4.0 %collective-permute-start.2 = (f16[64,512]{1,0:T(8,128)(2,1)S(1)}, f16[64,512]{1,0:T(8,128)(2,1)S(1)}, u32[]{:S(2)}, u32[]{:S(2)}) collective-permute-start(f16[64,512]{1,0:T(8,128)(2,1)S(1)} %pad_maximum_fusion.1), channel_id=1, source_target_pairs={{0,3},{1,2},{2,1},{3,0},{4,7},{5,6},{6,5},{7,4},{8,11},{9,10},{10,... | collective-permute-start | bytes 196616 | tf_op jit(solution)/shard_map/ppermute | solution.py:175
  11.1 3.5 %collective-permute-start.4 = (s32[32,512]{1,0:T(8,128)S(1)}, s32[32,512]{1,0:T(8,128)S(1)}, u32[]{:S(2)}, u32[]{:S(2)}) collective-permute-start(s32[32,512]{1,0:T(8,128)S(1)} %copy-done), channel_id=1, source_target_pairs={{0,1},{1,0},{2,3},{3,2},{4,5},{5,4},{6,7},{7,6},{8,9},{9,8},{10,11... | collective-permute-start | bytes 196616 | tf_op jit(solution)/shard_map/ppermute | solution.py:172
  13.3 4.4 %collective-permute-start.3 = (f16[128,512]{1,0:T(8,128)(2,1)S(1)}, f16[128,512]{1,0:T(8,128)(2,1)S(1)}, u32[]{:S(2)}, u32[]{:S(2)}) collective-permute-start(f16[128,512]{1,0:T(8,128)(2,1)S(1)} %pad_maximum_fusion), channel_id=1, source_target_pairs={{0,1},{1,0},{2,3},{3,2},{4,5},{5,4},{6,7},{7,6},{8,9},{9,8},{10,11... | collective-permute-start | bytes 393224 | tf_op jit(solution)/shard_map/ppermute | solution.py:175
  18.4 6.5 %collective-permute-start.5 = (f32[128,512]{1,0:T(8,128)S(1)}, f32[128,512]{1,0:T(8,128)S(1)}, u32[]{:S(2)}, u32[]{:S(2)}) collective-permute-start(f32[128,512]{1,0:T(8,128)S(1)} %shard_map.46), channel_id=1, source_target_pairs={{0,1},{1,0},{2,3},{3,2},{4,5},{5,4},{6,7},{7,6},{8,9},{9,8},{10,11... | collective-permute-start | bytes 786440 | tf_op jit(solution)/shard_map/ppermute | solution.py:188
  19.3 5.6 %collective-permute-start.6 = (f16[128,512]{1,0:T(8,128)(2,1)S(1)}, f16[128,512]{1,0:T(8,128)(2,1)S(1)}, u32[]{:S(2)}, u32[]{:S(2)}) collective-permute-start(f16[128,512]{1,0:T(8,128)(2,1)S(1)} %convert_element_type.34), channel_id=1, source_target_pairs={{0,17},{1,16},{2,19},{3,18},{4,21},{5,20},{6,23},{7,22},{8,25},{9,... | collective-permute-start | bytes 393224 | tf_op jit(solution)/shard_map/ppermute | solution.py:186

commit v7 on v6

--- a/solution.py
+++ b/solution.py
@@ -10,7 +10,7 @@
 SMALL = 2.0**-22
 RAISE_SMALL = 2.0**37
 RAISE = 2.0**8
-STRETCH = 163840.0
+STRETCH = 2.0**17
 CLOSE_BYTES = 1 << 19
 
 
@@ -148,9 +148,17 @@
 
 def distances_of(pick, queries, vectors, send):
     return pl.pallas_call(
-        lambda *refs: distance_kernel(send, *refs),
-        out_shape=result((pick.shape[0], vectors[0].shape[1]), jnp.float32),
+        lambda *refs: distance_kernel(send, *refs), out_shape=result((pick.shape[0], vectors[0].shape[1]), jnp.float32)
     )(*[in_vmem(array) for array in (pick, *queries, *vectors)])
+
+
+def round_queries(queries):
+    place = lax.broadcasted_iota(jnp.int32, queries.shape, 0) * queries.shape[1]
+    place = (place + lax.broadcasted_iota(jnp.int32, queries.shape, 1)).astype(jnp.float32) * 0.618034
+    offset = (place - jnp.floor(place)) * 2.0 - 1.0
+    stretched = queries * STRETCH
+    step = jnp.exp2(jnp.floor(jnp.log2(jnp.maximum(jnp.abs(stretched), 2.0**-14))) - 11.0)
+    return (stretched + offset * step).astype(jnp.float16)
 
 
 def split(rows):
@@ -170,7 +178,7 @@
         own_rows = queries.shape[0]
         mate = [(i, i ^ 1) for i in range(blocks)]
         code_ids = lax.ppermute(code_ids, "blk", mate)
-        rows = (queries * STRETCH).astype(jnp.float16)
+        rows = round_queries(queries)
         for step, mask in enumerate(masks):
             arrived = lax.ppermute(rows, "blk", [(i, i ^ mask) for i in range(blocks)])
             if step + 1 < len(masks):

time: 25.8 us -> 26 us (level)
  no operation moved by 1% of the time
where the time goes in v7:
time: 26 us; the launch traced here: 25.8 us
  starting transfers between devices  10.3 us (40%)
  waiting for transfers between devices  8.44 us (32%)
  Pallas kernels  5.12 us (20%)
  other arithmetic  1.78 us (7%)
    ppermute x4, starting transfers between devices, local(): arrived = lax.ppermute(rows, 'blk', [(i, i ^ mask) for i in range(blocks)])  7.68 us
    ppermute x4, waiting for transfers between devices, local(): arrived = lax.ppermute(rows, 'blk', [(i, i ^ mask) for i in range(blocks)])  4.84 us
    ppermute x1, waiting for transfers between devices, local(): arrived = lax.ppermute(theirs.astype(jnp.float16), ('sub', 'blk'), across)  3.59 us
    pallas_call x2, Pallas kernels, decode(): pl.pallas_call(lambda *refs: decode_kernel(part, *refs), in_specs=[pl.Blo...  3.09 us
    ppermute x1, starting transfers between devices, local(): arrived = lax.ppermute(theirs.astype(jnp.float16), ('sub', 'blk'), across)  2 us
    pallas_call x2, Pallas kernels, distances_of(): pl.pallas_call(lambda *refs: distance_kernel(send, *refs), out_shape=resu...  1.17 us
    pallas_call x1, Pallas kernels, make_picks(): pl.pallas_call(lambda *refs: pick_kernel(own_rows, masks, *refs), out_sha...  0.86 us
    convert_element_type x1, other arithmetic, round_queries(): return (stretched + offset * step).astype(jnp.float16)  0.84 us
  transfers between devices with their start and end apart: 7, of which 4 were waited for; matrix products, arithmetic and copies ran while one was open for 0% of the time, Pallas kernels for 18%

profile of v7, /device:TPU:0, one launch (start us, length us, event | category | flops | bytes accessed | tf_op | source)
XLA Modules:
  0.0 25.8 jit_solution(18080121982976167036)
XLA Ops:
  0.0 0.8 %fusion.7 = f16[16,512]{1,0:T(8,128)(2,1)S(1)} fusion(f32[16,512]{1,0:T(8,128)} %param.4, s32[16]{0:T(128)S(1)} %iota_multiply_fusion), kind=kLoop, calls=%fused_computation.16 | loop fusion | flops 139264 | bytes 49216 | tf_op jit(solution)/shard_map/convert_element_type | solution.py:161
  0.8 3.6 %collective-permute-start = (f16[16,512]{1,0:T(8,128)(2,1)S(1)}, f16[16,512]{1,0:T(8,128)(2,1)S(1)}, u32[]{:S(2)}, u32[]{:S(2)}) collective-permute-start(f16[16,512]{1,0:T(8,128)(2,1)S(1)} %fusion.7), channel_id=1, source_target_pairs={{0,9},{1,8},{2,11},{3,10},{4,13},{5,12},{6,15},{7,14},{8,1},{9,0},... | collective-permute-start | bytes 49160 | tf_op jit(solution)/shard_map/ppermute | solution.py:183
  4.4 1.4 %collective-permute-done = f16[16,512]{1,0:T(8,128)(2,1)S(1)} collective-permute-done((f16[16,512]{1,0:T(8,128)(2,1)S(1)}, f16[16,512]{1,0:T(8,128)(2,1)S(1)}, u32[]{:S(2)}, u32[]{:S(2)}) %collective-permute-start) | collective-permute-done | bytes 16416 | tf_op jit(solution)/shard_map/ppermute | solution.py:183
  5.9 0.0 copy-start
  5.9 2.0 %collective-permute-start.1 = (f16[32,512]{1,0:T(8,128)(2,1)S(1)}, f16[32,512]{1,0:T(8,128)(2,1)S(1)}, u32[]{:S(2)}, u32[]{:S(2)}) collective-permute-start(f16[32,512]{1,0:T(8,128)(2,1)S(1)} %pad_maximum_fusion.2), channel_id=1, source_target_pairs={{0,5},{1,4},{2,7},{3,6},{4,1},{5,0},{6,3},{7,2},{8,13},{9,12},{10,... | collective-permute-start | bytes 98312 | tf_op jit(solution)/shard_map/ppermute | solution.py:183
  7.8 1.6 %collective-permute-done.1 = f16[32,512]{1,0:T(8,128)(2,1)S(1)} collective-permute-done((f16[32,512]{1,0:T(8,128)(2,1)S(1)}, f16[32,512]{1,0:T(8,128)(2,1)S(1)}, u32[]{:S(2)}, u32[]{:S(2)}) %collective-permute-start.1) | collective-permute-done | bytes 32800 | tf_op jit(solution)/shard_map/ppermute | solution.py:183
  9.5 1.8 %collective-permute-start.2 = (f16[64,512]{1,0:T(8,128)(2,1)S(1)}, f16[64,512]{1,0:T(8,128)(2,1)S(1)}, u32[]{:S(2)}, u32[]{:S(2)}) collective-permute-start(f16[64,512]{1,0:T(8,128)(2,1)S(1)} %pad_maximum_fusion.1), channel_id=1, source_target_pairs={{0,3},{1,2},{2,1},{3,0},{4,7},{5,6},{6,5},{7,4},{8,11},{9,10},{10,... | collective-permute-start | bytes 196616 | tf_op jit(solution)/shard_map/ppermute | solution.py:183
  11.2 0.0 copy-done
  11.2 0.4 %collective-permute-start.4 = (s32[32,512]{1,0:T(8,128)S(1)}, s32[32,512]{1,0:T(8,128)S(1)}, u32[]{:S(2)}, u32[]{:S(2)}) collective-permute-start(s32[32,512]{1,0:T(8,128)S(1)} %copy-done), channel_id=1, source_target_pairs={{0,1},{1,0},{2,3},{3,2},{4,5},{5,4},{6,7},{7,6},{8,9},{9,8},{10,11... | collective-permute-start | bytes 196616 | tf_op jit(solution)/shard_map/ppermute | solution.py:180
  11.6 1.8 %collective-permute-done.2 = f16[64,512]{1,0:T(8,128)(2,1)S(1)} collective-permute-done((f16[64,512]{1,0:T(8,128)(2,1)S(1)}, f16[64,512]{1,0:T(8,128)(2,1)S(1)}, u32[]{:S(2)}, u32[]{:S(2)}) %collective-permute-start.2) | collective-permute-done | bytes 65568 | tf_op jit(solution)/shard_map/ppermute | solution.py:183
  13.5 0.4 %collective-permute-start.3 = (f16[128,512]{1,0:T(8,128)(2,1)S(1)}, f16[128,512]{1,0:T(8,128)(2,1)S(1)}, u32[]{:S(2)}, u32[]{:S(2)}) collective-permute-start(f16[128,512]{1,0:T(8,128)(2,1)S(1)} %pad_maximum_fusion), channel_id=1, source_target_pairs={{0,1},{1,0},{2,3},{3,2},{4,5},{5,4},{6,7},{7,6},{8,9},{9,8},{10,11... | collective-permute-start | bytes 393224 | tf_op jit(solution)/shard_map/ppermute | solution.py:183
  13.9 0.9 %picks.1 = (bf16[128,256]{1,0:T(8,128)(2,1)S(1)}, bf16[128,256]{1,0:T(8,128)(2,1)S(1)}) custom-call(s32[2,128]{1,0:T(2,128)} %bitcast.1), custom_call_target="tpu_custom_call" | custom-call | tf_op jit(solution)/shard_map/picks/pallas_call | solution.py:111
  14.7 0.0 collective-permute-done.4.refs_0_
  14.7 1.5 %decode.2 = (bf16[512,512]{1,0:T(8,128)(2,1)S(1)}, f32[8,512]{1,0:T(8,128)S(1)}) custom-call(s32[32,512]{1,0:T(8,128)S(1)} %collective-permute-done.4.refs_0_, f32[32,16,256]{2,1,0:T(8,128)} %refs_1_.3), custom_call_target="tpu_custom_call" | custom-call | tf_op jit(solution)/shard_map/decode/pallas_call | solution.py:80
  16.3 1.5 %decode.3 = (bf16[512,512]{1,0:T(8,128)(2,1)S(1)}, f32[8,512]{1,0:T(8,128)S(1)}) custom-call(s32[32,512]{1,0:T(8,128)S(1)} %collective-permute-done.4.refs_0_, f32[32,16,256]{2,1,0:T(8,128)} %refs_1_.3), custom_call_target="tpu_custom_call" | custom-call | tf_op jit(solution)/shard_map/decode/pallas_call | solution.py:80
  17.8 0.1 fusion.1
  17.9 0.0 collective-permute-done.3
  17.9 0.6 %shard_map.46 = f32[128,512]{1,0:T(8,128)S(1)} custom-call(bf16[128,256]{1,0:T(8,128)(2,1)S(1)} %get-tuple-element.11.refs_0_, bf16[128,512]{1,0:T(8,128)(2,1)S(1)} %get-tuple-element.20.refs_1_, bf16[128,512]{1,0:T(8,128)(2,1)S(1)} %get-tuple-element.19.refs_2_, bf16[128,512]{1,0:T(8,128)(2,1)S(1)} %get-tuple-element.18.refs_3_, ...), custom_call_target="tpu_custom_call" | custom-call | tf_op jit(solution)/shard_map/pallas_call | solution.py:150
  18.5 0.3 %collective-permute-start.5 = (f32[128,512]{1,0:T(8,128)S(1)}, f32[128,512]{1,0:T(8,128)S(1)}, u32[]{:S(2)}, u32[]{:S(2)}) collective-permute-start(f32[128,512]{1,0:T(8,128)S(1)} %shard_map.46), channel_id=1, source_target_pairs={{0,1},{1,0},{2,3},{3,2},{4,5},{5,4},{6,7},{7,6},{8,9},{9,8},{10,11... | collective-permute-start | bytes 786440 | tf_op jit(solution)/shard_map/ppermute | solution.py:196
  18.8 0.6 %shard_map.47 = f32[128,512]{1,0:T(8,128)S(1)} custom-call(bf16[128,256]{1,0:T(8,128)(2,1)S(1)} %get-tuple-element.16.refs_0_, bf16[128,512]{1,0:T(8,128)(2,1)S(1)} %get-tuple-element.20.refs_1_, bf16[128,512]{1,0:T(8,128)(2,1)S(1)} %get-tuple-element.19.refs_2_, bf16[128,512]{1,0:T(8,128)(2,1)S(1)} %get-tuple-element.18.refs_3_, ...), custom_call_target="tpu_custom_call" | custom-call | tf_op jit(solution)/shard_map/pallas_call | solution.py:150
  19.4 2.0 %collective-permute-start.6 = (f16[128,512]{1,0:T(8,128)(2,1)S(1)}, f16[128,512]{1,0:T(8,128)(2,1)S(1)}, u32[]{:S(2)}, u32[]{:S(2)}) collective-permute-start(f16[128,512]{1,0:T(8,128)(2,1)S(1)} %convert_element_type.38), channel_id=1, source_target_pairs={{0,17},{1,16},{2,19},{3,18},{4,21},{5,20},{6,23},{7,22},{8,25},{9,... | collective-permute-start | bytes 393224 | tf_op jit(solution)/shard_map/ppermute | solution.py:194
  21.4 3.6 %collective-permute-done.6 = f16[128,512]{1,0:T(8,128)(2,1)S(1)} collective-permute-done((f16[128,512]{1,0:T(8,128)(2,1)S(1)}, f16[128,512]{1,0:T(8,128)(2,1)S(1)}, u32[]{:S(2)}, u32[]{:S(2)}) %collective-permute-start.6) | collective-permute-done | bytes 131104 | tf_op jit(solution)/shard_map/ppermute | solution.py:194
  25.0 0.0 collective-permute-done.5
  25.0 0.7 %fusion = f32[128,512]{1,0:T(8,128)} fusion(f32[128,512]{1,0:T(8,128)S(1)} %collective-permute-done.5, f16[128,512]{1,0:T(8,128)(2,1)S(1)} %collective-permute-done.6), kind=kLoop, calls=%fused_computation.6 | loop fusion | flops 327680 | bytes 655360 | tf_op jit(solution)/shard_map/add | solution.py:198
  (6 shorter events, 0.1 us)
Async XLA Ops:
  0.8 5.0 %collective-permute-start = (f16[16,512]{1,0:T(8,128)(2,1)S(1)}, f16[16,512]{1,0:T(8,128)(2,1)S(1)}, u32[]{:S(2)}, u32[]{:S(2)}) collective-permute-start(f16[16,512]{1,0:T(8,128)(2,1)S(1)} %fusion.7), channel_id=1, source_target_pairs={{0,9},{1,8},{2,11},{3,10},{4,13},{5,12},{6,15},{7,14},{8,1},{9,0},... | collective-permute-start | bytes 49160 | tf_op jit(solution)/shard_map/ppermute | solution.py:183
  5.9 5.4 %copy-start = (s32[32,512]{1,0:T(8,128)S(1)}, s32[32,512]{1,0:T(8,128)}, u32[]{:S(2)}) copy-start(s32[32,512]{1,0:T(8,128)} %param.6) | copy-start | bytes 196612
  5.9 3.6 %collective-permute-start.1 = (f16[32,512]{1,0:T(8,128)(2,1)S(1)}, f16[32,512]{1,0:T(8,128)(2,1)S(1)}, u32[]{:S(2)}, u32[]{:S(2)}) collective-permute-start(f16[32,512]{1,0:T(8,128)(2,1)S(1)} %pad_maximum_fusion.2), channel_id=1, source_target_pairs={{0,5},{1,4},{2,7},{3,6},{4,1},{5,0},{6,3},{7,2},{8,13},{9,12},{10,... | collective-permute-start | bytes 98312 | tf_op jit(solution)/shard_map/ppermute | solution.py:183
  9.5 4.0 %collective-permute-start.2 = (f16[64,512]{1,0:T(8,128)(2,1)S(1)}, f16[64,512]{1,0:T(8,128)(2,1)S(1)}, u32[]{:S(2)}, u32[]{:S(2)}) collective-permute-start(f16[64,512]{1,0:T(8,128)(2,1)S(1)} %pad_maximum_fusion.1), channel_id=1, source_target_pairs={{0,3},{1,2},{2,1},{3,0},{4,7},{5,6},{6,5},{7,4},{8,11},{9,10},{10,... | collective-permute-start | bytes 196616 | tf_op jit(solution)/shard_map/ppermute | solution.py:183
  11.2 3.5 %collective-permute-start.4 = (s32[32,512]{1,0:T(8,128)S(1)}, s32[32,512]{1,0:T(8,128)S(1)}, u32[]{:S(2)}, u32[]{:S(2)}) collective-permute-start(s32[32,512]{1,0:T(8,128)S(1)} %copy-done), channel_id=1, source_target_pairs={{0,1},{1,0},{2,3},{3,2},{4,5},{5,4},{6,7},{7,6},{8,9},{9,8},{10,11... | collective-permute-start | bytes 196616 | tf_op jit(solution)/shard_map/ppermute | solution.py:180
  13.5 4.4 %collective-permute-start.3 = (f16[128,512]{1,0:T(8,128)(2,1)S(1)}, f16[128,512]{1,0:T(8,128)(2,1)S(1)}, u32[]{:S(2)}, u32[]{:S(2)}) collective-permute-start(f16[128,512]{1,0:T(8,128)(2,1)S(1)} %pad_maximum_fusion), channel_id=1, source_target_pairs={{0,1},{1,0},{2,3},{3,2},{4,5},{5,4},{6,7},{7,6},{8,9},{9,8},{10,11... | collective-permute-start | bytes 393224 | tf_op jit(solution)/shard_map/ppermute | solution.py:183
  18.5 6.5 %collective-permute-start.5 = (f32[128,512]{1,0:T(8,128)S(1)}, f32[128,512]{1,0:T(8,128)S(1)}, u32[]{:S(2)}, u32[]{:S(2)}) collective-permute-start(f32[128,512]{1,0:T(8,128)S(1)} %shard_map.46), channel_id=1, source_target_pairs={{0,1},{1,0},{2,3},{3,2},{4,5},{5,4},{6,7},{7,6},{8,9},{9,8},{10,11... | collective-permute-start | bytes 786440 | tf_op jit(solution)/shard_map/ppermute | solution.py:196
  19.4 5.6 %collective-permute-start.6 = (f16[128,512]{1,0:T(8,128)(2,1)S(1)}, f16[128,512]{1,0:T(8,128)(2,1)S(1)}, u32[]{:S(2)}, u32[]{:S(2)}) collective-permute-start(f16[128,512]{1,0:T(8,128)(2,1)S(1)} %convert_element_type.38), channel_id=1, source_target_pairs={{0,17},{1,16},{2,19},{3,18},{4,21},{5,20},{6,23},{7,22},{8,25},{9,... | collective-permute-start | bytes 393224 | tf_op jit(solution)/shard_map/ppermute | solution.py:194

commit v8 on v7

--- a/solution.py
+++ b/solution.py
@@ -112,24 +112,33 @@
         lambda *refs: pick_kernel(own_rows, masks, *refs),
         out_shape=(shape, shape),
         name="picks",
-    )(order)
-
-
-def picked(pick_ref, *row_refs):
-    total, first = None, 0
-    for row_ref in row_refs:
-        columns = pick_ref[:, pl.ds(first, row_ref.shape[0])]
-        rows = jnp.dot(columns, row_ref[...], preferred_element_type=jnp.float32)
-        total, first = rows if total is None else total + rows, first + row_ref.shape[0]
-    return total
+    )(in_vmem(order))
+
+
+def early_kernel(theirs_ref, mine_ref, high_ref, low_ref, *out_refs):
+    for side, pick_ref in enumerate((theirs_ref, mine_ref)):
+        pick = pick_ref[:, : high_ref.shape[0]]
+        for part, row_ref in enumerate((high_ref, low_ref)):
+            rows = jnp.dot(pick, row_ref[...], preferred_element_type=jnp.float32)
+            out_refs[2 * side + part][...] = rows.astype(jnp.bfloat16)
+
+
+def pick_early(pick_theirs, pick_mine, high, low):
+    shape = result((pick_mine.shape[0], high.shape[1]), jnp.bfloat16)
+    return pl.pallas_call(early_kernel, out_shape=(shape,) * 4, name="early")(
+        *[in_vmem(array) for array in (pick_theirs, pick_mine, high, low)]
+    )
 
 
 def distance_kernel(send, pick_ref, high_ref, low_ref, mate_high_ref, mate_low_ref, *refs):
-    high = picked(pick_ref, high_ref, mate_high_ref)
-    low = picked(pick_ref, low_ref, mate_low_ref)
-    whole = high + low
+    pick = pick_ref[:, pick_ref.shape[1] - mate_high_ref.shape[0] :]
+    high = jnp.dot(pick, mate_high_ref[...], preferred_element_type=jnp.float32)
+    low = jnp.dot(pick, mate_low_ref[...], preferred_element_type=jnp.float32)
+    high = high.astype(jnp.bfloat16) + high_ref[...]
+    low = low.astype(jnp.bfloat16) + low_ref[...]
+    whole = high.astype(jnp.float32) + low.astype(jnp.float32)
     rows = whole.shape[0]
-    both = jnp.concatenate([high, low], axis=0).astype(jnp.bfloat16)
+    both = jnp.concatenate([high, low], axis=0)
     cross = jnp.zeros((rows, refs[-1].shape[1]), jnp.float32)
     total = (1.0 / STRETCH**2) * jnp.sum(whole * whole, axis=1, keepdims=True)
     for part in range(PARTS):
@@ -184,15 +193,16 @@
             if step + 1 < len(masks):
                 rows = jnp.concatenate([rows, arrived], axis=0)
             else:
-                queries = (*split(rows), *split(arrived))
+                own, late = split(rows), split(arrived)
         pick_mine, pick_theirs = make_picks(own_rows, masks, query_order.reshape(halves, -1))
         vectors = []
         for part in range(PARTS):
             vectors.extend(decode(part, code_ids, centroids))
-        theirs = distances_of(pick_theirs, queries, vectors, True)
+        early = pick_early(pick_theirs, pick_mine, *own)
+        theirs = distances_of(pick_theirs, (*early[:2], *late), vectors, True)
         across = [(i, (i ^ 1) ^ blocks) for i in range(halves * blocks)]
         arrived = lax.ppermute(theirs.astype(jnp.float16), ("sub", "blk"), across)
-        mine = distances_of(pick_mine, queries, vectors, False)
+        mine = distances_of(pick_mine, (*early[2:], *late), vectors, False)
         mine = lax.ppermute(mine, "blk", mate)
         arrived = arrived.astype(jnp.float32)
         return mine + arrived * jnp.where(arrived < 0.0, -1.0 / RAISE_SMALL, 1.0 / RAISE)

time: 26 us -> 26.1 us (level)
  Pallas kernels: 5.12 us -> 4.57 us
  local copies, waits for them, and re-layouts: 0.01 us -> 0.3 us
    pallas_call x1, Pallas kernels: 0.86 us -> 0.18 us  [make_picks(): pl.pallas_call(lambda *refs: pick_kernel(own_rows, masks, *refs), out_sha...]
    unnamed x2 -> x4, local copies, waits for them, and re-layouts: 0.01 us -> 0.3 us
    pallas_call x0 -> x1, Pallas kernels: none -> 0.28 us  [pick_early(): pl.pallas_call(early_kernel, out_shape=(shape,) * 4, name='early')]
  transfers between devices with their start and end apart: 7 -> 7, of which waited for: 4 -> 4; matrix products, arithmetic and copies ran while one was open for 0% -> 0% of each run, Pallas kernels for 18% -> 16%
where the time goes in v8:
time: 26.1 us; the launch traced here: 25.9 us
  starting transfers between devices  10.5 us (40%)
  waiting for transfers between devices  8.6 us (33%)
  Pallas kernels  4.57 us (18%)
  other arithmetic  1.78 us (7%)
  local copies, waits for them, and re-layouts  0.3 us (1%)
    ppermute x4, starting transfers between devices, local(): arrived = lax.ppermute(rows, 'blk', [(i, i ^ mask) for i in range(blocks)])  7.68 us
    ppermute x4, waiting for transfers between devices, local(): arrived = lax.ppermute(rows, 'blk', [(i, i ^ mask) for i in range(blocks)])  4.84 us
    ppermute x1, waiting for transfers between devices, local(): arrived = lax.ppermute(theirs.astype(jnp.float16), ('sub', 'blk'), across)  3.76 us
    pallas_call x2, Pallas kernels, decode(): pl.pallas_call(lambda *refs: decode_kernel(part, *refs), in_specs=[pl.Blo...  3.1 us
    ppermute x1, starting transfers between devices, local(): arrived = lax.ppermute(theirs.astype(jnp.float16), ('sub', 'blk'), across)  2.09 us
    pallas_call x2, Pallas kernels, distances_of(): pl.pallas_call(lambda *refs: distance_kernel(send, *refs), out_shape=resu...  1.01 us
    convert_element_type x1, other arithmetic, round_queries(): return (stretched + offset * step).astype(jnp.float16)  0.84 us
    add x1, other arithmetic, local(): mine + arrived * jnp.where(arrived < 0.0, -1.0 / RAISE_SMALL, 1.0 / RAISE)  0.75 us
  transfers between devices with their start and end apart: 7, of which 4 were waited for; matrix products, arithmetic and copies ran while one was open for 0% of the time, Pallas kernels for 16%

profile of v8, /device:TPU:0, one launch (start us, length us, event | category | flops | bytes accessed | tf_op | source)
XLA Modules:
  0.0 25.9 jit_solution(16049343148773508198)
XLA Ops:
  0.0 0.8 %fusion.7 = f16[16,512]{1,0:T(8,128)(2,1)S(1)} fusion(f32[16,512]{1,0:T(8,128)} %param.4, s32[16]{0:T(128)S(1)} %iota_multiply_fusion), kind=kLoop, calls=%fused_computation.16 | loop fusion | flops 139264 | bytes 49216 | tf_op jit(solution)/shard_map/convert_element_type | solution.py:170
  0.8 3.6 %collective-permute-start = (f16[16,512]{1,0:T(8,128)(2,1)S(1)}, f16[16,512]{1,0:T(8,128)(2,1)S(1)}, u32[]{:S(2)}, u32[]{:S(2)}) collective-permute-start(f16[16,512]{1,0:T(8,128)(2,1)S(1)} %fusion.7), channel_id=1, source_target_pairs={{0,9},{1,8},{2,11},{3,10},{4,13},{5,12},{6,15},{7,14},{8,1},{9,0},... | collective-permute-start | bytes 49160 | tf_op jit(solution)/shard_map/ppermute | solution.py:192
  4.4 1.4 %collective-permute-done = f16[16,512]{1,0:T(8,128)(2,1)S(1)} collective-permute-done((f16[16,512]{1,0:T(8,128)(2,1)S(1)}, f16[16,512]{1,0:T(8,128)(2,1)S(1)}, u32[]{:S(2)}, u32[]{:S(2)}) %collective-permute-start) | collective-permute-done | bytes 16416 | tf_op jit(solution)/shard_map/ppermute | solution.py:192
  5.9 0.0 copy-start.1
  5.9 2.0 %collective-permute-start.1 = (f16[32,512]{1,0:T(8,128)(2,1)S(1)}, f16[32,512]{1,0:T(8,128)(2,1)S(1)}, u32[]{:S(2)}, u32[]{:S(2)}) collective-permute-start(f16[32,512]{1,0:T(8,128)(2,1)S(1)} %pad_maximum_fusion.2), channel_id=1, source_target_pairs={{0,5},{1,4},{2,7},{3,6},{4,1},{5,0},{6,3},{7,2},{8,13},{9,12},{10,... | collective-permute-start | bytes 98312 | tf_op jit(solution)/shard_map/ppermute | solution.py:192
  7.8 1.6 %collective-permute-done.1 = f16[32,512]{1,0:T(8,128)(2,1)S(1)} collective-permute-done((f16[32,512]{1,0:T(8,128)(2,1)S(1)}, f16[32,512]{1,0:T(8,128)(2,1)S(1)}, u32[]{:S(2)}, u32[]{:S(2)}) %collective-permute-start.1) | collective-permute-done | bytes 32800 | tf_op jit(solution)/shard_map/ppermute | solution.py:192
  9.5 1.8 %collective-permute-start.2 = (f16[64,512]{1,0:T(8,128)(2,1)S(1)}, f16[64,512]{1,0:T(8,128)(2,1)S(1)}, u32[]{:S(2)}, u32[]{:S(2)}) collective-permute-start(f16[64,512]{1,0:T(8,128)(2,1)S(1)} %pad_maximum_fusion.1), channel_id=1, source_target_pairs={{0,3},{1,2},{2,1},{3,0},{4,7},{5,6},{6,5},{7,4},{8,11},{9,10},{10,... | collective-permute-start | bytes 196616 | tf_op jit(solution)/shard_map/ppermute | solution.py:192
  11.2 0.4 %collective-permute-start.4 = (s32[32,512]{1,0:T(8,128)S(1)}, s32[32,512]{1,0:T(8,128)S(1)}, u32[]{:S(2)}, u32[]{:S(2)}) collective-permute-start(s32[32,512]{1,0:T(8,128)S(1)} %copy-done.1), channel_id=1, source_target_pairs={{0,1},{1,0},{2,3},{3,2},{4,5},{5,4},{6,7},{7,6},{8,9},{9,8},{10,11... | collective-permute-start | bytes 196616 | tf_op jit(solution)/shard_map/ppermute | solution.py:189
  11.6 1.8 %collective-permute-done.2 = f16[64,512]{1,0:T(8,128)(2,1)S(1)} collective-permute-done((f16[64,512]{1,0:T(8,128)(2,1)S(1)}, f16[64,512]{1,0:T(8,128)(2,1)S(1)}, u32[]{:S(2)}, u32[]{:S(2)}) %collective-permute-start.2) | collective-permute-done | bytes 65568 | tf_op jit(solution)/shard_map/ppermute | solution.py:192
  13.5 0.0 copy-start
  13.5 0.4 %collective-permute-start.3 = (f16[128,512]{1,0:T(8,128)(2,1)S(1)}, f16[128,512]{1,0:T(8,128)(2,1)S(1)}, u32[]{:S(2)}, u32[]{:S(2)}) collective-permute-start(f16[128,512]{1,0:T(8,128)(2,1)S(1)} %pad_maximum_fusion), channel_id=1, source_target_pairs={{0,1},{1,0},{2,3},{3,2},{4,5},{5,4},{6,7},{7,6},{8,9},{9,8},{10,11... | collective-permute-start | bytes 393224 | tf_op jit(solution)/shard_map/ppermute | solution.py:192
  13.9 0.3 %copy-done = s32[256]{0:T(256)S(1)} copy-done((s32[256]{0:T(256)S(1)}, s32[256]{0:T(256)}, u32[]{:S(2)}) %copy-start) | copy-done | bytes 1048
  14.2 0.2 picks.1
  14.3 0.0 collective-permute-done.4.refs_0_
  14.3 1.5 %decode.3 = (bf16[512,512]{1,0:T(8,128)(2,1)S(1)}, f32[8,512]{1,0:T(8,128)S(1)}) custom-call(s32[32,512]{1,0:T(8,128)S(1)} %collective-permute-done.4.refs_0_, f32[32,16,256]{2,1,0:T(8,128)} %refs_1_.3), custom_call_target="tpu_custom_call" | custom-call | tf_op jit(solution)/shard_map/decode/pallas_call | solution.py:80
  15.9 1.5 %decode.2 = (bf16[512,512]{1,0:T(8,128)(2,1)S(1)}, f32[8,512]{1,0:T(8,128)S(1)}) custom-call(s32[32,512]{1,0:T(8,128)S(1)} %collective-permute-done.4.refs_0_, f32[32,16,256]{2,1,0:T(8,128)} %refs_1_.3), custom_call_target="tpu_custom_call" | custom-call | tf_op jit(solution)/shard_map/decode/pallas_call | solution.py:80
  17.5 0.1 fusion.1
  17.5 0.3 %early.1 = (bf16[128,512]{1,0:T(8,128)(2,1)S(1)}, bf16[128,512]{1,0:T(8,128)(2,1)S(1)}, bf16[128,512]{1,0:T(8,128)(2,1)S(1)}, bf16[128,512]{1,0:T(8,128)(2,1)S(1)}) custom-call(bf16[128,256]{1,0:T(8,128)(2,1)S(1)} %get-tuple-element.16.theirs_ref.refs_0_, bf16[128,256]{1,0:T(8,128)(2,1)S(1)} %get-tuple-element.15.mine_ref.refs_0_, ...), custom_call_target="tpu_custom_call" | custom-call | tf_op jit(solution)/shard_map/early/pallas_call | solution.py:128
  17.9 0.5 %shard_map.46 = f32[128,512]{1,0:T(8,128)S(1)} custom-call(bf16[128,256]{1,0:T(8,128)(2,1)S(1)} %get-tuple-element.15.mine_ref.refs_0_, bf16[128,512]{1,0:T(8,128)(2,1)S(1)} %get-tuple-element.17.refs_1_, bf16[128,512]{1,0:T(8,128)(2,1)S(1)} %get-tuple-element.18.refs_2_, bf16[128,512]{1,0:T(8,128)(2,1)S(1)} %get-tuple-element.26.refs_3_, ...), custom_call_target="tpu_custom_call" | custom-call | tf_op jit(solution)/shard_map/pallas_call | solution.py:159
  18.4 0.4 %collective-permute-start.5 = (f32[128,512]{1,0:T(8,128)S(1)}, f32[128,512]{1,0:T(8,128)S(1)}, u32[]{:S(2)}, u32[]{:S(2)}) collective-permute-start(f32[128,512]{1,0:T(8,128)S(1)} %shard_map.46), channel_id=1, source_target_pairs={{0,1},{1,0},{2,3},{3,2},{4,5},{5,4},{6,7},{7,6},{8,9},{9,8},{10,11... | collective-permute-start | bytes 786440 | tf_op jit(solution)/shard_map/ppermute | solution.py:206
  18.7 0.5 %shard_map.47 = f32[128,512]{1,0:T(8,128)S(1)} custom-call(bf16[128,256]{1,0:T(8,128)(2,1)S(1)} %get-tuple-element.16.theirs_ref.refs_0_, bf16[128,512]{1,0:T(8,128)(2,1)S(1)} %get-tuple-element.23.refs_1_, bf16[128,512]{1,0:T(8,128)(2,1)S(1)} %get-tuple-element.24.refs_2_, bf16[128,512]{1,0:T(8,128)(2,1)S(1)} %get-tuple-element.26.refs_3_, ...), custom_call_target="tpu_custom_call" | custom-call | tf_op jit(solution)/shard_map/pallas_call | solution.py:159
  19.3 2.1 %collective-permute-start.6 = (f16[128,512]{1,0:T(8,128)(2,1)S(1)}, f16[128,512]{1,0:T(8,128)(2,1)S(1)}, u32[]{:S(2)}, u32[]{:S(2)}) collective-permute-start(f16[128,512]{1,0:T(8,128)(2,1)S(1)} %convert_element_type.38), channel_id=1, source_target_pairs={{0,17},{1,16},{2,19},{3,18},{4,21},{5,20},{6,23},{7,22},{8,25},{9,... | collective-permute-start | bytes 393224 | tf_op jit(solution)/shard_map/ppermute | solution.py:204
  21.4 3.8 %collective-permute-done.6 = f16[128,512]{1,0:T(8,128)(2,1)S(1)} collective-permute-done((f16[128,512]{1,0:T(8,128)(2,1)S(1)}, f16[128,512]{1,0:T(8,128)(2,1)S(1)}, u32[]{:S(2)}, u32[]{:S(2)}) %collective-permute-start.6) | collective-permute-done | bytes 131104 | tf_op jit(solution)/shard_map/ppermute | solution.py:204
  25.2 0.7 %fusion = f32[128,512]{1,0:T(8,128)} fusion(f32[128,512]{1,0:T(8,128)S(1)} %collective-permute-done.5, f16[128,512]{1,0:T(8,128)(2,1)S(1)} %collective-permute-done.6), kind=kLoop, calls=%fused_computation.6 | loop fusion | flops 327680 | bytes 655360 | tf_op jit(solution)/shard_map/add | solution.py:208
  (9 shorter events, 0.1 us)
Async XLA Ops:
  0.8 5.0 %collective-permute-start = (f16[16,512]{1,0:T(8,128)(2,1)S(1)}, f16[16,512]{1,0:T(8,128)(2,1)S(1)}, u32[]{:S(2)}, u32[]{:S(2)}) collective-permute-start(f16[16,512]{1,0:T(8,128)(2,1)S(1)} %fusion.7), channel_id=1, source_target_pairs={{0,9},{1,8},{2,11},{3,10},{4,13},{5,12},{6,15},{7,14},{8,1},{9,0},... | collective-permute-start | bytes 49160 | tf_op jit(solution)/shard_map/ppermute | solution.py:192
  5.9 5.4 %copy-start.1 = (s32[32,512]{1,0:T(8,128)S(1)}, s32[32,512]{1,0:T(8,128)}, u32[]{:S(2)}) copy-start(s32[32,512]{1,0:T(8,128)} %param.6) | copy-start | bytes 196612
  5.9 3.6 %collective-permute-start.1 = (f16[32,512]{1,0:T(8,128)(2,1)S(1)}, f16[32,512]{1,0:T(8,128)(2,1)S(1)}, u32[]{:S(2)}, u32[]{:S(2)}) collective-permute-start(f16[32,512]{1,0:T(8,128)(2,1)S(1)} %pad_maximum_fusion.2), channel_id=1, source_target_pairs={{0,5},{1,4},{2,7},{3,6},{4,1},{5,0},{6,3},{7,2},{8,13},{9,12},{10,... | collective-permute-start | bytes 98312 | tf_op jit(solution)/shard_map/ppermute | solution.py:192
  9.5 4.0 %collective-permute-start.2 = (f16[64,512]{1,0:T(8,128)(2,1)S(1)}, f16[64,512]{1,0:T(8,128)(2,1)S(1)}, u32[]{:S(2)}, u32[]{:S(2)}) collective-permute-start(f16[64,512]{1,0:T(8,128)(2,1)S(1)} %pad_maximum_fusion.1), channel_id=1, source_target_pairs={{0,3},{1,2},{2,1},{3,0},{4,7},{5,6},{6,5},{7,4},{8,11},{9,10},{10,... | collective-permute-start | bytes 196616 | tf_op jit(solution)/shard_map/ppermute | solution.py:192
  11.2 3.1 %collective-permute-start.4 = (s32[32,512]{1,0:T(8,128)S(1)}, s32[32,512]{1,0:T(8,128)S(1)}, u32[]{:S(2)}, u32[]{:S(2)}) collective-permute-start(s32[32,512]{1,0:T(8,128)S(1)} %copy-done.1), channel_id=1, source_target_pairs={{0,1},{1,0},{2,3},{3,2},{4,5},{5,4},{6,7},{7,6},{8,9},{9,8},{10,11... | collective-permute-start | bytes 196616 | tf_op jit(solution)/shard_map/ppermute | solution.py:189
  13.5 0.7 %copy-start = (s32[256]{0:T(256)S(1)}, s32[256]{0:T(256)}, u32[]{:S(2)}) copy-start(s32[256]{0:T(256)} %param.7) | copy-start | bytes 3076
  13.5 4.3 %collective-permute-start.3 = (f16[128,512]{1,0:T(8,128)(2,1)S(1)}, f16[128,512]{1,0:T(8,128)(2,1)S(1)}, u32[]{:S(2)}, u32[]{:S(2)}) collective-permute-start(f16[128,512]{1,0:T(8,128)(2,1)S(1)} %pad_maximum_fusion), channel_id=1, source_target_pairs={{0,1},{1,0},{2,3},{3,2},{4,5},{5,4},{6,7},{7,6},{8,9},{9,8},{10,11... | collective-permute-start | bytes 393224 | tf_op jit(solution)/shard_map/ppermute | solution.py:192
  18.4 6.8 %collective-permute-start.5 = (f32[128,512]{1,0:T(8,128)S(1)}, f32[128,512]{1,0:T(8,128)S(1)}, u32[]{:S(2)}, u32[]{:S(2)}) collective-permute-start(f32[128,512]{1,0:T(8,128)S(1)} %shard_map.46), channel_id=1, source_target_pairs={{0,1},{1,0},{2,3},{3,2},{4,5},{5,4},{6,7},{7,6},{8,9},{9,8},{10,11... | collective-permute-start | bytes 786440 | tf_op jit(solution)/shard_map/ppermute | solution.py:206
  19.3 5.9 %collective-permute-start.6 = (f16[128,512]{1,0:T(8,128)(2,1)S(1)}, f16[128,512]{1,0:T(8,128)(2,1)S(1)}, u32[]{:S(2)}, u32[]{:S(2)}) collective-permute-start(f16[128,512]{1,0:T(8,128)(2,1)S(1)} %convert_element_type.38), channel_id=1, source_target_pairs={{0,17},{1,16},{2,19},{3,18},{4,21},{5,20},{6,23},{7,22},{8,25},{9,... | collective-permute-start | bytes 393224 | tf_op jit(solution)/shard_map/ppermute | solution.py:204
